TPU v7x, 128 devices: a whole 4x4x4 slice. The times are simulated.
128 devices in a mesh: dp: 8 (over x, core), tensor: 16 (over z, y).
Axes of the slice: x: 4, y: 4, z: 4, core: 2. Of those that a mesh axis runs over, the one named last changes fastest.
Arguments:
- tokens: bfloat16 [192, 8, 4096], P('dp'), may hold values from -6 to 6
- norm_gain: float32 [4096], replicated, may hold values from 0.1 to 1.9
- in_weight: bfloat16 [4096, 2, 8192], P(None, None, 'tensor'), may hold values from -0.09375 to 0.09375
- group_weight: bfloat16 [4096, 2048], P(None, 'tensor'), may hold values from -0.09375 to 0.09375
- step_weight: bfloat16 [4096, 128], P(None, 'tensor'), may hold values from -0.09375 to 0.09375
- value_kernel: bfloat16 [4, 8192], P(None, 'tensor'), may hold values from -3 to 3
- value_offset: bfloat16 [8192], P('tensor'), may hold values from -3 to 3
- group_kernel: bfloat16 [4, 2048], P(None, 'tensor'), may hold values from -3 to 3
- group_offset: bfloat16 [2048], P('tensor'), may hold values from -3 to 3
- step_bias: float32 [128], P('tensor'), may hold values from -4 to 1
- decay_rate: float32 [128], P('tensor'), may hold values from 0.05 to 2
- skip_gain: float32 [128], P('tensor'), may hold values from 0.5 to 2
- out_gain: float32 [8192], P('tensor'), may hold values from 0.1 to 1.9
- out_weight: bfloat16 [8192, 4096], P('tensor'), may hold values from -0.0625 to 0.0625
- scan_state: bfloat16 [192, 128, 64, 128], P('dp', 'tensor'), may hold values from -6 to 6
- value_cache: bfloat16 [192, 3, 8192], P('dp', None, 'tensor'), may hold values from -6 to 6
- group_cache: bfloat16 [192, 3, 2048], P('dp', None, 'tensor'), may hold values from -6 to 6
- accepted: int32 [192], P('dp'), may hold values from 0 to 8, as said below
- draft_lengths: int32 [192], P('dp'), may hold values from 1 to 8, as said below
- live_flags: int32 [192], P('dp'), may hold values 0 or 1
Outputs:
- layer_out: bfloat16 [192, 8, 4096], P('dp')
- kept_state: bfloat16 [192, 128, 64, 128], P('dp', 'tensor')
- value_kept: bfloat16 [192, 3, 8192], P('dp', None, 'tensor')
- group_kept: bfloat16 [192, 3, 2048], P('dp', None, 'tensor')
- accepted_total: int32 [1], replicated
Inputs may be any that keep to these rules, and one draw needn't show every extreme that they name: `draft_lengths`: positions at or after a request's draft length are padding. `accepted`: never more than the same request's draft length.
All inputs are finite; a program needn't handle non-finite values.
Results may differ from a plain program's by a relative error of at most 0.012.
Values may be sent and summed in bfloat16 or wider, within the bound.
No kernel may reach another device: no remote copies, remote signals or barrier semaphores. Data moves between devices by JAX's collectives and lax.ppermute only.
A program may use at most 128 MiB of HBM per device.

v0:
```python
import math

import jax
import jax.numpy as jnp
from jax import lax
from jax.experimental import pallas as pl
from jax.experimental.pallas import tpu as pltpu
from jax.sharding import Mesh
from jax.sharding import PartitionSpec as P

DP = ("dp_0", "dp_1")


EPSILON = 1e-05


ALL = ("dp_0", "dp_1", "tensor")
NEAR = (0, 1, 4, 5)
FAR = (0, 3, 12, 15)
COLS = 256
AHEAD = 2


def swapped(value, axis, mask):
    pairs = [(source, source ^ mask) for source in range(math.prod(lax.axis_size(a) for a in axis))]
    return lax.ppermute(value, axis, pairs)


def exchanged(value, masks):
    tensor = lax.axis_size("tensor")
    total = tensor * lax.axis_size("dp_0") * lax.axis_size("dp_1")
    pairs = [(s, s ^ masks[(s // tensor) % 2]) for s in range(total)]
    return lax.ppermute(value, ALL, pairs)


def chunk_at(outer, inner):
    me = lax.axis_index("tensor")
    core = lax.axis_index("dp_1")
    near = (me ^ (me >> 1)) & 5
    even = near ^ (NEAR[outer] ^ FAR[inner])
    odd = me ^ near ^ (FAR[outer] ^ NEAR[inner])
    return jnp.where(core == 0, even, odd)


def group_scale(own_squares, other_squares, channels):
    return lax.rsqrt((own_squares + other_squares) / channels + EPSILON)


def out_project(gated, out_weight, outers, squares=()):
    rows, inner_dev = gated.shape
    given = len(squares)
    count = len(outers)
    width = 4 * COLS

    def body(gated_ref, weight_ref, *rest):
        parts, (buffer, sems) = rest[given : given + count], rest[given + count :]

        def copies_of(turn):
            copies = []
            for inner in range(4):
                start = pl.multiple_of(chunk_at(outers[turn], inner) * COLS, COLS)
                copies.append(
                    pltpu.make_async_copy(
                        weight_ref.at[:, pl.ds(start, COLS)],
                        buffer.at[turn, :, pl.ds(inner * COLS, COLS)],
                        sems.at[turn, inner],
                    )
                )
            return copies

        copies = [copies_of(turn) for turn in range(count)]
        for turn in range(count):
            for copy in copies[turn]:
                copy.start()
        for turn in range(count):
            for copy in copies[turn]:
                copy.wait()
            part = jnp.dot(gated_ref[...], buffer[turn], preferred_element_type=jnp.float32)
            if given:
                part = part * group_scale(rest[0][...], rest[1][...], 2 * inner_dev)
            part = part.astype(jnp.bfloat16)
            for inner in range(4):
                parts[turn][inner] = part[:, inner * COLS : (inner + 1) * COLS]

    whole = pl.BlockSpec(memory_space=pltpu.VMEM)
    return pl.pallas_call(
        body,
        out_shape=[jax.ShapeDtypeStruct((4, rows, COLS), jnp.bfloat16)] * count,
        in_specs=[whole, pl.BlockSpec(memory_space=pl.ANY)] + [whole] * given,
        out_specs=[whole] * count,
        scratch_shapes=[
            pltpu.VMEM((count, inner_dev, width), jnp.bfloat16),
            pltpu.SemaphoreType.DMA((count, 4)),
        ],
        name="out_project",
    )(gated, out_weight, *squares)


def placed(pieces, outers, earlier=None):
    rows = pieces[0].shape[1]
    count = len(pieces)

    def body(*refs):
        sources, (out_ref, sems) = refs[:count], refs[-2:]
        copies = []
        for index, outer in enumerate(outers):
            for inner in range(4):
                start = pl.multiple_of(chunk_at(outer, inner) * COLS, COLS)
                copies.append(
                    pltpu.make_async_copy(
                        sources[index].at[inner],
                        out_ref.at[:, pl.ds(start, COLS)],
                        sems.at[index, inner],
                    )
                )
        for copy in copies:
            copy.start()
        for copy in copies:
            copy.wait()

    operands = list(pieces) + ([] if earlier is None else [earlier])
    return pl.pallas_call(
        body,
        out_shape=jax.ShapeDtypeStruct((rows, 16 * COLS), jnp.bfloat16),
        in_specs=[pl.BlockSpec(memory_space=pltpu.VMEM)] * count
        + [pl.BlockSpec(memory_space=pl.ANY)] * (len(operands) - count),
        out_specs=pl.BlockSpec(memory_space=pl.ANY),
        scratch_shapes=[pltpu.SemaphoreType.DMA((count, 4))],
        input_output_aliases={} if earlier is None else {count: 0},
        name="place_rows",
    )(*operands)


def added(own, received):
    wide = [piece.astype(jnp.float32) for piece in (own, *received)]
    return ((wide[0] + wide[1]) + (wide[2] + wide[3])).astype(jnp.bfloat16)


def stage(pieces, first, second, steps=(3, 2, 1)):
    masks = list(zip(first, second))
    return {step: exchanged(pieces[step], masks[step]) for step in steps}


def silu(value):
    return value / (1.0 + jnp.exp(-value))


def shifted_conv(fresh, cache_ref, kernel_ref, offset_ref):
    position = lax.broadcasted_iota(jnp.int32, fresh.shape, 1)
    kernel = kernel_ref[...].astype(jnp.float32)
    cache = [cache_ref[i].astype(jnp.float32)[:, None, :] for i in range(3)]
    summed = fresh * kernel[3:4][None] + offset_ref[...].astype(jnp.float32).reshape(1, 1, -1)
    for back in (1, 2, 3):
        moved = pltpu.roll(fresh, back, axis=1)
        for place in range(back):
            moved = jnp.where(position == place, cache[3 - back + place], moved)
        summed = summed + moved * kernel[3 - back : 4 - back][None]
    return silu(summed)


def enter(tokens, norm_gain, group_weight, step_weight, group_cache, group_kernel, group_offset):
    rows, width = tokens.shape
    cols = group_weight.shape[1]
    heads = step_weight.shape[0]

    def body(
        tok_ref, gain_ref, gw_ref, sw_ref, cache_ref, ker_ref, off_ref,
        normed_ref, proj_ref, conv_ref, step_ref,
    ):
        wide = tok_ref[...].astype(jnp.float32)
        scale = lax.rsqrt(jnp.mean(wide * wide, axis=1, keepdims=True) + EPSILON)
        normed = (wide * scale * gain_ref[...]).astype(jnp.bfloat16)
        normed_ref[...] = normed
        proj = jnp.dot(normed, gw_ref[...], preferred_element_type=jnp.float32)
        proj = proj.astype(jnp.bfloat16)
        proj_ref[...] = proj
        step_ref[...] = lax.dot_general(
            normed, sw_ref[...], (((1,), (1,)), ((), ())), preferred_element_type=jnp.float32
        )
        fresh = proj.astype(jnp.float32).reshape(rows // 8, 8, cols)
        conv_ref[...] = shifted_conv(fresh, cache_ref, ker_ref, off_ref).astype(jnp.bfloat16)

    whole = pl.BlockSpec(memory_space=pltpu.VMEM)
    return pl.pallas_call(
        body,
        out_shape=[
            jax.ShapeDtypeStruct((rows, width), jnp.bfloat16),
            jax.ShapeDtypeStruct((rows, cols), jnp.bfloat16),
            jax.ShapeDtypeStruct((rows // 8, 8, cols), jnp.bfloat16),
            jax.ShapeDtypeStruct((rows, heads), jnp.float32),
        ],
        in_specs=[whole] * 7,
        out_specs=[whole] * 4,
        name="enter",
    )(tokens, norm_gain, group_weight, step_weight, group_cache, group_kernel, group_offset)


def in_project(normed, in_weight):
    rows, width = normed.shape
    half = width // 2
    lane_blocks = in_weight.shape[2] // 128
    inner_dev = in_weight.shape[2]
    pairs = lane_blocks // 2
    halves = 2
    depth = half // halves
    viewed = in_weight.reshape(half, 2, 2, lane_blocks, 128).transpose(0, 1, 3, 2, 4)

    def body(normed_ref, weight_ref, gate_ref, value_ref, buffer, left, sems):
        def copies_of(turn):
            pair, part = turn
            span = pl.ds(part * depth, depth)
            return [
                pltpu.make_async_copy(
                    weight_ref.at[span, parity, block],
                    buffer.at[parity, block, span],
                    sems.at[part, parity, block],
                )
                for parity in range(2)
                for block in (2 * pair, 2 * pair + 1)
            ]

        turns = [(pair, part) for pair in range(pairs) for part in range(halves)]
        for turn in turns[:AHEAD]:
            for copy in copies_of(turn):
                copy.start()
        flat = buffer.reshape(2 * lane_blocks * width, 128)
        even = lax.broadcasted_iota(jnp.int32, (rows, 128), 1) % 2 == 0
        for lane in range(0, width, 128):
            span = slice(lane, lane + 128)
            piece = normed_ref[:, span].astype(jnp.float32)
            first = jnp.where(even, piece, 0.0)
            second = jnp.where(even, 0.0, piece)
            left[0, 0:rows, span] = first.astype(jnp.bfloat16)
            left[0, rows:, span] = pltpu.roll(first, 1, axis=1).astype(jnp.bfloat16)
            left[1, 0:rows, span] = pltpu.roll(second, 127, axis=1).astype(jnp.bfloat16)
            left[1, rows:, span] = second.astype(jnp.bfloat16)
        total = None
        for index, (pair, part) in enumerate(turns):
            for copy in copies_of((pair, part)):
                copy.wait()
            if index + AHEAD < len(turns):
                for copy in copies_of(turns[index + AHEAD]):
                    copy.start()
            for parity in range(2):
                right = jnp.concatenate(
                    [
                        flat[pl.ds((parity * lane_blocks + block) * width + 2 * depth * part, 2 * depth)]
                        for block in (2 * pair, 2 * pair + 1)
                    ],
                    axis=1,
                )
                product = jnp.dot(
                    left[parity, :, 2 * depth * part : 2 * depth * (part + 1)],
                    right,
                    preferred_element_type=jnp.float32,
                )
                total = product if total is None else total + product
            if part == halves - 1:
                span = slice(256 * pair, 256 * pair + 256)
                gate_ref[:, span] = total[:rows].astype(jnp.bfloat16)
                value_ref[:, span] = total[rows:].astype(jnp.bfloat16)
                total = None

    whole = pl.BlockSpec(memory_space=pltpu.VMEM)
    return pl.pallas_call(
        body,
        out_shape=[jax.ShapeDtypeStruct((rows, inner_dev), jnp.bfloat16)] * 2,
        in_specs=[whole, pl.BlockSpec(memory_space=pl.ANY)],
        out_specs=[whole] * 2,
        scratch_shapes=[
            pltpu.VMEM((2, lane_blocks, half, 2, 128), jnp.bfloat16),
            pltpu.VMEM((2, 2 * rows, width), jnp.bfloat16),
            pltpu.SemaphoreType.DMA((halves, 2, lane_blocks)),
        ],
        name="in_project",
    )(normed, viewed)


def recur(
    gate, value, value_cache, value_kernel, value_offset, step_raw, step_bias, decay_rate,
    skip_gain, out_gain, own_map, other_map, accepted, draft_lengths, live_flags, scan_state,
):
    rows, inner_dev = gate.shape
    requests = rows // 8
    heads = step_raw.shape[1]
    head_dim = inner_dev // heads
    each = 12

    def body(
        gate_ref, value_ref, cache_ref, ker_ref, off_ref, raw_ref, bias_ref, rate_ref, skip_ref,
        gain_ref, own_ref, other_ref, accepted_ref, length_ref, live_ref, state_ref,
        gated_ref, square_ref, weighted_ref, decay_ref,
        x_buf, step_buf, after_buf, skip_buf, narrow_buf,
    ):
        turn = pl.program_id(0)
        first_half = lax.axis_index("tensor") % 2 == 0

        @pl.when(turn == 0)
        def _():
            fresh = value_ref[...].astype(jnp.float32).reshape(requests, 8, inner_dev)
            x_buf[...] = shifted_conv(fresh, cache_ref, ker_ref, off_ref)
            raw = raw_ref[...] + bias_ref[...]
            step = jnp.maximum(raw, 0.0) + jnp.log1p(jnp.exp(-jnp.abs(raw)))
            after = (-step * rate_ref[...]).reshape(requests, 8, heads)
            place = lax.broadcasted_iota(jnp.int32, after.shape, 1)
            for back in (1, 2, 4):
                after = after + jnp.where(place >= back, pltpu.roll(after, back, axis=1), 0.0)
            spread = (
                lax.broadcasted_iota(jnp.int32, (heads, inner_dev), 1) // head_dim
                == lax.broadcasted_iota(jnp.int32, (heads, inner_dev), 0)
            ).astype(jnp.float32)

            def widened(narrow):
                return jnp.dot(
                    narrow, spread, precision=lax.Precision.HIGHEST,
                    preferred_element_type=jnp.float32,
                )

            step_buf[...] = widened(step).reshape(requests, 8, inner_dev)
            after_buf[...] = widened(after.reshape(rows, heads)).reshape(requests, 8, inner_dev)
            skip_buf[...] = widened(jnp.broadcast_to(skip_ref[...], (8, heads)))
            narrow_buf[...] = after

        position = lax.broadcasted_iota(jnp.int32, (8, inner_dev), 0)
        skip = skip_buf[0:1]
        for index in range(each):
            request = turn * each + index
            span = pl.ds(request * 8, 8)
            after = after_buf[request]
            x = x_buf[request]
            pushed = step_buf[request] * x
            own, other = own_ref[request], other_ref[request]
            reads = jnp.where(first_half, other, own)
            writes = jnp.where(first_half, own, other)
            state = state_ref[index]
            across = (((1,), (1,)), ((), ()))
            carried = lax.dot_general(reads, state, across, preferred_element_type=jnp.float32)
            aligned = lax.dot_general(reads, writes, across, preferred_element_type=jnp.float32)
            total = carried * jnp.exp(after) + skip * x
            for source in range(8):
                gap = jnp.where(position >= source, after - after[source : source + 1], -1e30)
                total = total + jnp.exp(gap) * (
                    aligned[:, source : source + 1] * pushed[source : source + 1]
                )
            gated = total * silu(gate_ref[span].astype(jnp.float32))
            square_ref[span] = jnp.sum(gated * gated, axis=1, keepdims=True)
            length = jnp.where(live_ref[request] == 1, length_ref[request], 0)
            gated = jnp.where(position < length, gated * gain_ref[...], 0.0)
            gated_ref[span] = gated.astype(jnp.bfloat16)
            kept = accepted_ref[request] * live_ref[request]
            narrow = narrow_buf[request]
            place = lax.broadcasted_iota(jnp.int32, narrow.shape, 0)
            narrow = jnp.sum(jnp.where(place == kept - 1, narrow, 0.0), axis=0, keepdims=True)
            decay_ref[pl.ds(request, 1)] = jnp.exp(narrow)
            end = jnp.sum(jnp.where(position == kept - 1, after, 0.0), axis=0, keepdims=True)
            gap = jnp.where(position < kept, end - after, -1e30)
            weighted_ref[request] = (jnp.exp(gap) * pushed).astype(jnp.bfloat16)

    whole = pl.BlockSpec(memory_space=pltpu.VMEM)
    return pl.pallas_call(
        body,
        grid=(requests // each,),
        out_shape=[
            jax.ShapeDtypeStruct((rows, inner_dev), jnp.bfloat16),
            jax.ShapeDtypeStruct((rows, 1), jnp.float32),
            jax.ShapeDtypeStruct((requests, 8, inner_dev), jnp.bfloat16),
            jax.ShapeDtypeStruct((requests, heads), jnp.float32),
        ],
        in_specs=[whole] * 12
        + [pl.BlockSpec(memory_space=pltpu.SMEM)] * 3
        + [pl.BlockSpec((each, inner_dev, 128), lambda turn: (turn, 0, 0))],
        out_specs=[whole] * 4,
        scratch_shapes=[
            pltpu.VMEM((requests, 8, inner_dev), jnp.float32),
            pltpu.VMEM((requests, 8, inner_dev), jnp.float32),
            pltpu.VMEM((requests, 8, inner_dev), jnp.float32),
            pltpu.VMEM((8, inner_dev), jnp.float32),
            pltpu.VMEM((requests, 8, heads), jnp.float32),
        ],
        name="recur",
    )(
        gate, value, value_cache, value_kernel, value_offset, step_raw, step_bias, decay_rate,
        skip_gain, out_gain, own_map, other_map, accepted, draft_lengths, live_flags, scan_state,
    )


def keep_window(sequence, kept_count, width_rows):
    return jax.vmap(
        lambda single, start_row: lax.dynamic_slice_in_dim(single, start_row, width_rows, 0)
    )(sequence, kept_count)


def local(
    tokens,
    norm_gain,
    in_weight,
    group_weight,
    step_weight,
    value_kernel,
    value_offset,
    group_kernel,
    group_offset,
    step_bias,
    decay_rate,
    skip_gain,
    out_gain,
    out_weight,
    scan_state,
    value_cache,
    group_cache,
    accepted,
    draft_lengths,
    live_flags,
):
    requests, positions, model_width = tokens.shape
    row_total = requests * positions
    inner_dev = value_offset.shape[0]
    tap_count = value_kernel.shape[0]
    kept_count = accepted * live_flags
    parity = lax.axis_index("tensor") % 2
    normed, group_proj, own_conv, step_raw = enter(
        tokens.reshape(row_total, model_width),
        norm_gain[None],
        group_weight,
        step_weight.T,
        group_cache.transpose(1, 0, 2),
        group_kernel,
        group_offset[None],
    )
    other_conv = swapped(own_conv, ("tensor",), 1)
    gate_part, value_part = in_project(normed, in_weight)
    input_map = jnp.where(parity == 0, own_conv, other_conv)
    scaled, own_squares, weighted, kept_decay = recur(
        gate_part,
        value_part,
        value_cache.transpose(1, 0, 2),
        value_kernel,
        value_offset,
        step_raw,
        step_bias[None],
        decay_rate[None],
        skip_gain[None],
        out_gain[None],
        own_conv,
        other_conv,
        accepted,
        draft_lengths,
        live_flags,
        scan_state.reshape(requests, inner_dev, scan_state.shape[3]),
    )
    other_squares = swapped(own_squares, ("tensor",), 1)
    (raw,) = out_project(scaled, out_weight, (3,))
    squares = (own_squares, other_squares)
    scale = group_scale(*squares, 2 * inner_dev)
    farthest = (raw.astype(jnp.float32) * scale).astype(jnp.bfloat16)
    received = stage({3: farthest}, NEAR, FAR, (3,))
    scaled, farthest = lax.optimization_barrier((scaled, farthest))
    second, first, own = out_project(scaled, out_weight, (2, 1, 0), squares)
    own, value_part, group_proj = lax.optimization_barrier((own, value_part, group_proj))
    received.update(stage({2: second, 1: first}, NEAR, FAR, (2, 1)))
    count = jnp.sum(kept_count).reshape(1)
    count, own = lax.optimization_barrier((count, own))
    count = count + swapped(count, DP, 1)
    reduced = added(own, [received[step] for step in (1, 2, 3)])
    count, reduced = lax.optimization_barrier((count, reduced))
    count = count + swapped(count, DP, 2)
    received = stage([reduced] * 4, FAR, NEAR)
    accepted_total = count + swapped(count, DP, 6)
    accepted_total, received[1] = lax.optimization_barrier((accepted_total, received[1]))
    finished = added(reduced, [received[step] for step in (1, 2, 3)])
    finished, weighted = lax.optimization_barrier((finished, weighted))
    received = stage([finished] * 4, NEAR, FAR)
    layer_rows = placed([finished, received[3]], (0, 3))
    layer_rows = placed([received[2], received[1]], (2, 1), layer_rows)
    kept_state = (
        kept_decay[:, :, None, None] * scan_state.astype(jnp.float32)
        + jnp.einsum(
            "rjq,rjn->rqn", weighted, input_map, preferred_element_type=jnp.float32
        ).reshape(scan_state.shape)
    ).astype(jnp.bfloat16)
    value_seq = jnp.concatenate(
        [value_cache, value_part.reshape(requests, positions, inner_dev)], axis=1
    )
    group_seq = jnp.concatenate(
        [group_cache, group_proj.reshape(requests, positions, -1)], axis=1
    )
    value_kept = keep_window(value_seq, kept_count, tap_count - 1)
    group_kept = keep_window(group_seq, kept_count, tap_count - 1)
    return (
        layer_rows.reshape(requests, positions, model_width),
        kept_state,
        value_kept,
        group_kept,
        accepted_total,
    )


def solution(mesh):
    torus = Mesh(mesh.devices.reshape(4, 2, mesh.shape["tensor"]), ("dp_0", "dp_1", "tensor"))
    in_specs = (
        P(DP, None, None),
        P(),
        P(None, None, "tensor"),
        P(None, "tensor"),
        P(None, "tensor"),
        P(None, "tensor"),
        P("tensor"),
        P(None, "tensor"),
        P("tensor"),
        P("tensor"),
        P("tensor"),
        P("tensor"),
        P("tensor"),
        P("tensor", None),
        P(DP, "tensor", None, None),
        P(DP, None, "tensor"),
        P(DP, None, "tensor"),
        P(DP),
        P(DP),
        P(DP),
    )
    out_specs = (
        P(DP, None, None),
        P(DP, "tensor", None, None),
        P(DP, None, "tensor"),
        P(DP, None, "tensor"),
        P(),
    )
    return jax.shard_map(local, mesh=torus, in_specs=in_specs, out_specs=out_specs, check_vma=False)
```

profile of v0, /device:TPU:12, one launch (start us, length us, event | category | flops | bytes accessed | tf_op | source)
XLA Modules:
  0.0 87.9 jit_solution(5541263415500037127)
XLA Ops:
  0.6 3.9 %enter.1 = (bf16[192,4096]{1,0:T(8,128)(2,1)}, bf16[192,128]{1,0:T(8,128)(2,1)}, bf16[24,8,128]{2,1,0:T(8,128)(2,1)}, f32[192,8]{1,0:T(8,128)}) custom-call(bf16[192,4096]{1,0:T(8,128)(2,1)} %bitcast.32, f32[1,4096]{1,0:T(1,128)} %bitcast.38, bf16[4096,128]{1,0:T(8,128)(2,1)} %gw_ref.1, bf16[8,4096]{1,0:T(8,128)(2,1)} %bitcast.36, ...), custom_call_target="tpu_custom_call" | custom-call | tf_op jit(solution)/shard_map/enter/pallas_call | solution.py:184
  5.0 10.7 %in_project.1 = (bf16[192,512]{1,0:T(8,128)(2,1)}, bf16[192,512]{1,0:T(8,128)(2,1)}) custom-call(bf16[192,4096]{1,0:T(8,128)(2,1)} %get-tuple-element.30.normed_ref, bf16[2048,2,4,2,128]{4,3,2,1,0:T(2,128)(2,1)} %bitcast.30), custom_call_target="tpu_custom_call" | custom-call | tf_op jit(solution)/shard_map/in_project/pallas_call | solution.py:265
  16.3 5.5 %recur.1 = (bf16[192,512]{1,0:T(8,128)(2,1)}, f32[192,1]{1,0:T(8,128)}, bf16[24,8,512]{2,1,0:T(8,128)(2,1)}, f32[24,8]{1,0:T(8,128)}) custom-call(bf16[192,512]{1,0:T(8,128)(2,1)} %get-tuple-element.31.gate_ref, bf16[192,512]{1,0:T(8,128)(2,1)} %get-tuple-element.52.value_ref, bf16[3,24,512]{2,1,0:T(8,128)(2,1)} %bitcast.34, bf16[4,512]{1,0:T(4,128)(2,1)} %ker_ref.3, ...), custom_call_target="tpu_custom_call" | custom-call | tf_op jit(solution)/shard_map/recur/pallas_call | solution.py:360
  21.8 1.8 %collective-permute-start.1 = (f32[192,1]{1,0:T(8,128)}, f32[192,1]{1,0:T(8,128)S(1)}, u32[]{:S(2)}, u32[]{:S(2)}) collective-permute-start(f32[192,1]{1,0:T(8,128)} %get-tuple-element.36.rest_0_), channel_id=1, source_target_pairs={{0,1},{1,0},{2,3},{3,2},{4,5},{5,4},{6,7},{7,6},{8,9},{9,8},{10,11... | collective-permute-start | bytes 2312 | tf_op jit(solution)/shard_map/ppermute | solution.py:26
  23.7 3.3 %out_project.2 = bf16[4,192,256]{2,1,0:T(8,128)(2,1)} custom-call(bf16[192,512]{1,0:T(8,128)(2,1)} %get-tuple-element.37.gated_ref, bf16[512,4096]{1,0:T(8,128)(2,1)} %weight_ref.3), custom_call_target="tpu_custom_call" | custom-call | tf_op jit(solution)/shard_map/out_project/pallas_call | solution.py:86
  27.2 1.1 %multiply_convert_fusion = bf16[4,192,256]{2,1,0:T(8,128)(2,1)S(1)} fusion(bf16[4,192,256]{2,1,0:T(8,128)(2,1)} %out_project.2, f32[192]{0:T(256)S(1)} %rsqrt_reduce_fusion), kind=kLoop, calls=%fused_computation.5 | loop fusion | flops 589824 | bytes 787200 | tf_op jit(solution)/shard_map/convert_element_type | solution.py:455
  28.4 4.3 %out_project.3 = (bf16[4,192,256]{2,1,0:T(8,128)(2,1)}, bf16[4,192,256]{2,1,0:T(8,128)(2,1)}, bf16[4,192,256]{2,1,0:T(8,128)(2,1)}) custom-call(bf16[192,512]{1,0:T(8,128)(2,1)} %get-tuple-element.37.gated_ref, bf16[512,4096]{1,0:T(8,128)(2,1)} %weight_ref.3, f32[192,1]{1,0:T(8,128)} %get-tuple-element.36.rest_0_, f32[192,1]{1,0:T(8,128)} %copy-done.5), custom_call_target="tpu_custom_call" | custom-call | tf_op jit(solution)/shard_map/out_project/pallas_call | solution.py:86
  32.7 1.5 %collective-permute-start.3 = (bf16[4,192,256]{2,1,0:T(8,128)(2,1)}, bf16[4,192,256]{2,1,0:T(8,128)(2,1)S(1)}, u32[]{:S(2)}, u32[]{:S(2)}) collective-permute-start(bf16[4,192,256]{2,1,0:T(8,128)(2,1)} %get-tuple-element.43), channel_id=1, source_target_pairs={{0,1},{1,0},{2,3},{3,2},{4,5},{5,4},{6,7},{7,6},{8,9},{9,8},{10,11... | collective-permute-start | bytes 1179656 | tf_op jit(solution)/shard_map/ppermute | solution.py:33
  34.2 1.9 %collective-permute-start.4 = (bf16[4,192,256]{2,1,0:T(8,128)(2,1)}, bf16[4,192,256]{2,1,0:T(8,128)(2,1)S(1)}, u32[]{:S(2)}, u32[]{:S(2)}) collective-permute-start(bf16[4,192,256]{2,1,0:T(8,128)(2,1)} %get-tuple-element.44), channel_id=1, source_target_pairs={{0,4},{1,5},{2,6},{3,7},{4,0},{5,1},{6,2},{7,3},{8,12},{9,13},{10,... | collective-permute-start | bytes 1179656 | tf_op jit(solution)/shard_map/ppermute | solution.py:33
  36.9 0.8 collective-permute-start.2
  37.7 1.0 %collective-permute-done.2 = s32[1]{0:T(128)} collective-permute-done((s32[1]{0:T(128)}, s32[1]{0:T(128)}, u32[]{:S(2)}, u32[]{:S(2)}) %collective-permute-start.2) | collective-permute-done | bytes 36 | tf_op jit(solution)/shard_map/ppermute | solution.py:26
  40.0 0.7 collective-permute-done.3
  40.7 5.2 %collective-permute-done.4 = bf16[4,192,256]{2,1,0:T(8,128)(2,1)S(1)} collective-permute-done((bf16[4,192,256]{2,1,0:T(8,128)(2,1)}, bf16[4,192,256]{2,1,0:T(8,128)(2,1)S(1)}, u32[]{:S(2)}, u32[]{:S(2)}) %collective-permute-start.4) | collective-permute-done | bytes 393248 | tf_op jit(solution)/shard_map/ppermute | solution.py:33
  46.4 1.2 %add_convert_fusion.2 = bf16[4,192,256]{2,1,0:T(8,128)(2,1)S(1)} fusion(bf16[4,192,256]{2,1,0:T(8,128)(2,1)S(1)} %collective-permute-done.5, bf16[4,192,256]{2,1,0:T(8,128)(2,1)S(1)} %collective-permute-done.4, bf16[4,192,256]{2,1,0:T(8,128)(2,1)S(1)} %collective-permute-done.3, bf16[4,192,256]{2,1,0:T(8,128)(2,1)} %get-tuple-element.42), kind=kLoop, calls=%fused_computation.4 | loop fusion | flops 1572864 | bytes 1966080 | tf_op jit(solution)/shard_map/convert_element_type | solution.py:136
  47.6 2.3 %collective-permute-start.8 = (bf16[4,192,256]{2,1,0:T(8,128)(2,1)S(1)}, bf16[4,192,256]{2,1,0:T(8,128)(2,1)S(1)}, u32[]{:S(2)}, u32[]{:S(2)}) collective-permute-start(bf16[4,192,256]{2,1,0:T(8,128)(2,1)S(1)} %add_convert_fusion.2), channel_id=1, source_target_pairs={{0,3},{1,2},{2,1},{3,0},{4,7},{5,6},{6,5},{7,4},{8,11},{9,10},{10,... | collective-permute-start | bytes 1179656 | tf_op jit(solution)/shard_map/ppermute | solution.py:33
  49.8 3.3 %collective-permute-start.10 = (bf16[4,192,256]{2,1,0:T(8,128)(2,1)S(1)}, bf16[4,192,256]{2,1,0:T(8,128)(2,1)S(1)}, u32[]{:S(2)}, u32[]{:S(2)}) collective-permute-start(bf16[4,192,256]{2,1,0:T(8,128)(2,1)S(1)} %add_convert_fusion.2), channel_id=1, source_target_pairs={{0,15},{1,14},{2,13},{3,12},{4,11},{5,10},{6,9},{7,8},{8,7},{9,6},... | collective-permute-start | bytes 1179656 | tf_op jit(solution)/shard_map/ppermute | solution.py:33
  53.4 1.6 %gather_fusion = bf16[24,3,512]{2,0,1:T(8,128)(2,1)} fusion(bf16[24,11,512]{2,0,1:T(8,128)(2,1)S(1)} %pad_maximum_fusion, s32[24]{0:T(128)S(1)} %fusion.7), kind=kCustom, calls=%fused_computation | custom fusion | bytes 147744 | tf_op jit(solution)/shard_map/vmap()/gather | solution.py:389
  55.1 1.4 %gather_fusion.1 = bf16[24,3,128]{2,0,1:T(8,128)(2,1)} fusion(bf16[24,11,128]{2,0,1:T(8,128)(2,1)S(1)} %pad_maximum_fusion.1, s32[24]{0:T(128)S(1)} %fusion.7), kind=kCustom, calls=%fused_computation.1 | custom fusion | bytes 37152 | tf_op jit(solution)/shard_map/vmap()/gather | solution.py:389
  56.5 2.5 %collective-permute-start.6 = (s32[1]{0:T(128)}, s32[1]{0:T(128)}, u32[]{:S(2)}, u32[]{:S(2)}) collective-permute-start(s32[1]{0:T(128)} %add.52), channel_id=1, source_target_pairs={{0,32},{16,48},{32,0},{48,16},{64,96},{80,112},{96,64},{112,80},{1... | collective-permute-start | bytes 20 | tf_op jit(solution)/shard_map/ppermute | solution.py:26
  59.0 1.0 %collective-permute-done.6 = s32[1]{0:T(128)} collective-permute-done((s32[1]{0:T(128)}, s32[1]{0:T(128)}, u32[]{:S(2)}, u32[]{:S(2)}) %collective-permute-start.6) | collective-permute-done | bytes 36 | tf_op jit(solution)/shard_map/ppermute | solution.py:26
  60.6 1.9 %collective-permute-start.7 = (s32[1]{0:T(128)}, s32[1]{0:T(128)}, u32[]{:S(2)}, u32[]{:S(2)}) collective-permute-start(s32[1]{0:T(128)} %add.56), channel_id=1, source_target_pairs={{0,96},{16,112},{32,64},{48,80},{64,32},{80,48},{96,0},{112,16},{1... | collective-permute-start | bytes 20 | tf_op jit(solution)/shard_map/ppermute | solution.py:26
  62.5 1.7 %collective-permute-done.7 = s32[1]{0:T(128)} collective-permute-done((s32[1]{0:T(128)}, s32[1]{0:T(128)}, u32[]{:S(2)}, u32[]{:S(2)}) %collective-permute-start.7) | collective-permute-done | bytes 36 | tf_op jit(solution)/shard_map/ppermute | solution.py:26
  64.9 5.9 %collective-permute-done.9 = bf16[4,192,256]{2,1,0:T(8,128)(2,1)S(1)} collective-permute-done((bf16[4,192,256]{2,1,0:T(8,128)(2,1)S(1)}, bf16[4,192,256]{2,1,0:T(8,128)(2,1)S(1)}, u32[]{:S(2)}, u32[]{:S(2)}) %collective-permute-start.9) | collective-permute-done | bytes 393248 | tf_op jit(solution)/shard_map/ppermute | solution.py:33
  71.2 3.4 %collective-permute-start.12 = (bf16[4,192,256]{2,1,0:T(8,128)(2,1)S(1)}, bf16[4,192,256]{2,1,0:T(8,128)(2,1)S(1)}, u32[]{:S(2)}, u32[]{:S(2)}) collective-permute-start(bf16[4,192,256]{2,1,0:T(8,128)(2,1)S(1)} %add_convert_fusion.1.refs_0_), channel_id=1, source_target_pairs={{0,1},{1,0},{2,3},{3,2},{4,5},{5,4},{6,7},{7,6},{8,9},{9,8},{10,11... | collective-permute-start | bytes 1179656 | tf_op jit(solution)/shard_map/ppermute | solution.py:33
  74.6 1.1 %fusion = f32[24,512,128]{2,1,0:T(8,128)S(1)} fusion(bf16[24,8,512]{2,1,0:T(8,128)(2,1)S(1)} %copy-done.12, bf16[24,8,128]{2,1,0:T(8,128)(2,1)S(1)} %copy-done.9, bf16[24,8,128]{2,1,0:T(8,128)(2,1)S(1)} %copy-done.11, pred[]{:T(512)S(6)} %eq.5), kind=kOutput, calls=%fused_computation.9 | convolution fusion | flops 25190400 | bytes 6586369 | tf_op jit(solution)/shard_map/rjq,rjn->rqn/dot_general | solution.py:477
  75.7 2.6 %add_convert_fusion = bf16[24,8,64,128]{3,2,1,0:T(8,128)(2,1)} fusion(f32[24,8,64,128]{3,2,1,0:T(8,128)S(1)} %bitcast.28, bf16[24,8,64,128]{3,2,1,0:T(8,128)(2,1)S(1)} %copy-done, f32[24,8]{1,0:T(8,128)S(1)} %copy-done.15), kind=kLoop, calls=%fused_computation.2 | loop fusion | flops 6291456 | bytes 12583680 | tf_op jit(solution)/shard_map/convert_element_type | solution.py:480
  78.2 1.6 %collective-permute-done.13.refs_1_ = bf16[4,192,256]{2,1,0:T(8,128)(2,1)S(1)} collective-permute-done((bf16[4,192,256]{2,1,0:T(8,128)(2,1)S(1)}, bf16[4,192,256]{2,1,0:T(8,128)(2,1)S(1)}, u32[]{:S(2)}, u32[]{:S(2)}) %collective-permute-start.13) | collective-permute-done | bytes 393248 | tf_op jit(solution)/shard_map/ppermute | solution.py:33
  79.9 0.8 copy-done.3
  80.6 2.0 %place_rows.2.refs_2_ = bf16[192,4096]{1,0:T(8,128)(2,1)} custom-call(bf16[4,192,256]{2,1,0:T(8,128)(2,1)} %copy-done.1, bf16[4,192,256]{2,1,0:T(8,128)(2,1)} %copy-done.3), custom_call_target="tpu_custom_call" | custom-call | tf_op jit(solution)/shard_map/place_rows/pallas_call | solution.py:122
  83.2 0.8 copy-done.6
  83.9 0.8 copy-done.7
  84.7 2.0 %place_rows.3 = bf16[192,4096]{1,0:T(8,128)(2,1)} custom-call(bf16[4,192,256]{2,1,0:T(8,128)(2,1)} %copy-done.6, bf16[4,192,256]{2,1,0:T(8,128)(2,1)} %copy-done.7, bf16[192,4096]{1,0:T(8,128)(2,1)} %place_rows.2.refs_2_), custom_call_target="tpu_custom_call", output_to_operand_aliasing={{}: (2, {})} | custom-call | tf_op jit(solution)/shard_map/place_rows/pallas_call | solution.py:122
  (53 shorter events, 3.6 us)
Async XLA Ops:
  4.5 11.2 %collective-permute-start = (bf16[24,8,128]{2,1,0:T(8,128)(2,1)}, bf16[24,8,128]{2,1,0:T(8,128)(2,1)S(1)}, u32[]{:S(2)}, u32[]{:S(2)}) collective-permute-start(bf16[24,8,128]{2,1,0:T(8,128)(2,1)} %get-tuple-element.34.own_ref), channel_id=1, source_target_pairs={{0,1},{1,0},{2,3},{3,2},{4,5},{5,4},{6,7},{7,6},{8,9},{9,8},{10,11... | collective-permute-start | bytes 147464 | tf_op jit(solution)/shard_map/ppermute | solution.py:26
  15.7 0.6 copy-start.10
  21.8 5.2 %copy-start.4 = (f32[192,1]{1,0:T(8,128)S(1)}, f32[192,1]{1,0:T(8,128)}, u32[]{:S(2)}) copy-start(f32[192,1]{1,0:T(8,128)} %get-tuple-element.36.rest_0_) | copy-start | bytes 2308
  21.8 5.2 %collective-permute-start.1 = (f32[192,1]{1,0:T(8,128)}, f32[192,1]{1,0:T(8,128)S(1)}, u32[]{:S(2)}, u32[]{:S(2)}) collective-permute-start(f32[192,1]{1,0:T(8,128)} %get-tuple-element.36.rest_0_), channel_id=1, source_target_pairs={{0,1},{1,0},{2,3},{3,2},{4,5},{5,4},{6,7},{7,6},{8,9},{9,8},{10,11... | collective-permute-start | bytes 2312 | tf_op jit(solution)/shard_map/ppermute | solution.py:26
  23.7 12.6 %copy-start.16 = (s32[24]{0:T(128)S(1)}, s32[24]{0:T(128)}, u32[]{:S(2)}) copy-start(s32[24]{0:T(128)} %accepted_ref.1) | copy-start | bytes 292
  23.7 12.6 %copy-start.17 = (s32[24]{0:T(128)S(1)}, s32[24]{0:T(128)}, u32[]{:S(2)}) copy-start(s32[24]{0:T(128)} %live_ref.1) | copy-start | bytes 292
  27.0 26.3 %copy-start.2 = (bf16[192,512]{1,0:T(8,128)(2,1)S(1)}, bf16[192,512]{1,0:T(8,128)(2,1)}, u32[]{:S(2)}) copy-start(bf16[192,512]{1,0:T(8,128)(2,1)} %get-tuple-element.52.value_ref) | copy-start | bytes 589828
  27.0 26.3 %copy-start.14 = (bf16[192,128]{1,0:T(8,128)(2,1)S(1)}, bf16[192,128]{1,0:T(8,128)(2,1)}, u32[]{:S(2)}) copy-start(bf16[192,128]{1,0:T(8,128)(2,1)} %get-tuple-element.53) | copy-start | bytes 147460
  27.0 26.4 %copy-start.8 = (bf16[24,3,512]{2,0,1:T(8,128)(2,1)S(1)}, bf16[24,3,512]{2,0,1:T(8,128)(2,1)}, u32[]{:S(2)}) copy-start(bf16[24,3,512]{2,0,1:T(8,128)(2,1)} %param.35) | copy-start | bytes 221188
  27.1 1.3 %copy-start.5 = (f32[192,1]{1,0:T(8,128)}, f32[192,1]{1,0:T(8,128)S(1)}, u32[]{:S(2)}) copy-start(f32[192,1]{1,0:T(8,128)S(1)} %collective-permute-done.1.rest_1_) | copy-start | bytes 2308
  28.3 26.7 %copy-start.13 = (bf16[24,3,128]{2,0,1:T(8,128)(2,1)S(1)}, bf16[24,3,128]{2,0,1:T(8,128)(2,1)}, u32[]{:S(2)}) copy-start(bf16[24,3,128]{2,0,1:T(8,128)(2,1)} %param.36) | copy-start | bytes 55300
  32.6 42.0 %copy-start.9 = (bf16[24,8,128]{2,1,0:T(8,128)(2,1)S(1)}, bf16[24,8,128]{2,1,0:T(8,128)(2,1)}, u32[]{:S(2)}) copy-start(bf16[24,8,128]{2,1,0:T(8,128)(2,1)} %get-tuple-element.34.own_ref) | copy-start | bytes 147460
  32.6 41.9 %copy-start.11 = (bf16[24,8,128]{2,1,0:T(8,128)(2,1)S(1)}, bf16[24,8,128]{2,1,0:T(8,128)(2,1)}, u32[]{:S(2)}) copy-start(bf16[24,8,128]{2,1,0:T(8,128)(2,1)} %copy-done.10) | copy-start | bytes 147460
  32.7 41.9 %copy-start.12 = (bf16[24,8,512]{2,1,0:T(8,128)(2,1)S(1)}, bf16[24,8,512]{2,1,0:T(8,128)(2,1)}, u32[]{:S(2)}) copy-start(bf16[24,8,512]{2,1,0:T(8,128)(2,1)} %get-tuple-element.51) | copy-start | bytes 589828
  32.7 8.1 %collective-permute-start.3 = (bf16[4,192,256]{2,1,0:T(8,128)(2,1)}, bf16[4,192,256]{2,1,0:T(8,128)(2,1)S(1)}, u32[]{:S(2)}, u32[]{:S(2)}) collective-permute-start(bf16[4,192,256]{2,1,0:T(8,128)(2,1)} %get-tuple-element.43), channel_id=1, source_target_pairs={{0,1},{1,0},{2,3},{3,2},{4,5},{5,4},{6,7},{7,6},{8,9},{9,8},{10,11... | collective-permute-start | bytes 1179656 | tf_op jit(solution)/shard_map/ppermute | solution.py:33
  34.2 11.7 %collective-permute-start.4 = (bf16[4,192,256]{2,1,0:T(8,128)(2,1)}, bf16[4,192,256]{2,1,0:T(8,128)(2,1)S(1)}, u32[]{:S(2)}, u32[]{:S(2)}) collective-permute-start(bf16[4,192,256]{2,1,0:T(8,128)(2,1)} %get-tuple-element.44), channel_id=1, source_target_pairs={{0,4},{1,5},{2,6},{3,7},{4,0},{5,1},{6,2},{7,3},{8,12},{9,13},{10,... | collective-permute-start | bytes 1179656 | tf_op jit(solution)/shard_map/ppermute | solution.py:33
  36.1 10.3 %collective-permute-start.5 = (bf16[4,192,256]{2,1,0:T(8,128)(2,1)S(1)}, bf16[4,192,256]{2,1,0:T(8,128)(2,1)S(1)}, u32[]{:S(2)}, u32[]{:S(2)}) collective-permute-start(bf16[4,192,256]{2,1,0:T(8,128)(2,1)S(1)} %multiply_convert_fusion), channel_id=1, source_target_pairs={{0,5},{1,4},{2,7},{3,6},{4,1},{5,0},{6,3},{7,2},{8,13},{9,12},{10,... | collective-permute-start | bytes 1179656 | tf_op jit(solution)/shard_map/ppermute | solution.py:33
  36.9 1.8 %collective-permute-start.2 = (s32[1]{0:T(128)}, s32[1]{0:T(128)}, u32[]{:S(2)}, u32[]{:S(2)}) collective-permute-start(s32[1]{0:T(128)} %bitcast), channel_id=1, source_target_pairs={{0,16},{16,0},{32,48},{48,32},{64,80},{80,64},{96,112},{112,96},{1... | collective-permute-start | bytes 20 | tf_op jit(solution)/shard_map/ppermute | solution.py:26
  47.6 17.3 %collective-permute-start.8 = (bf16[4,192,256]{2,1,0:T(8,128)(2,1)S(1)}, bf16[4,192,256]{2,1,0:T(8,128)(2,1)S(1)}, u32[]{:S(2)}, u32[]{:S(2)}) collective-permute-start(bf16[4,192,256]{2,1,0:T(8,128)(2,1)S(1)} %add_convert_fusion.2), channel_id=1, source_target_pairs={{0,3},{1,2},{2,1},{3,0},{4,7},{5,6},{6,5},{7,4},{8,11},{9,10},{10,... | collective-permute-start | bytes 1179656 | tf_op jit(solution)/shard_map/ppermute | solution.py:33
  49.8 15.1 %collective-permute-start.10 = (bf16[4,192,256]{2,1,0:T(8,128)(2,1)S(1)}, bf16[4,192,256]{2,1,0:T(8,128)(2,1)S(1)}, u32[]{:S(2)}, u32[]{:S(2)}) collective-permute-start(bf16[4,192,256]{2,1,0:T(8,128)(2,1)S(1)} %add_convert_fusion.2), channel_id=1, source_target_pairs={{0,15},{1,14},{2,13},{3,12},{4,11},{5,10},{6,9},{7,8},{8,7},{9,6},... | collective-permute-start | bytes 1179656 | tf_op jit(solution)/shard_map/ppermute | solution.py:33
  53.2 17.6 %collective-permute-start.9 = (bf16[4,192,256]{2,1,0:T(8,128)(2,1)S(1)}, bf16[4,192,256]{2,1,0:T(8,128)(2,1)S(1)}, u32[]{:S(2)}, u32[]{:S(2)}) collective-permute-start(bf16[4,192,256]{2,1,0:T(8,128)(2,1)S(1)} %add_convert_fusion.2), channel_id=1, source_target_pairs={{0,12},{1,13},{2,14},{3,15},{4,8},{5,9},{6,10},{7,11},{8,4},{9,5},... | collective-permute-start | bytes 1179656 | tf_op jit(solution)/shard_map/ppermute | solution.py:33
  56.5 3.5 %collective-permute-start.6 = (s32[1]{0:T(128)}, s32[1]{0:T(128)}, u32[]{:S(2)}, u32[]{:S(2)}) collective-permute-start(s32[1]{0:T(128)} %add.52), channel_id=1, source_target_pairs={{0,32},{16,48},{32,0},{48,16},{64,96},{80,112},{96,64},{112,80},{1... | collective-permute-start | bytes 20 | tf_op jit(solution)/shard_map/ppermute | solution.py:26
  60.6 3.6 %collective-permute-start.7 = (s32[1]{0:T(128)}, s32[1]{0:T(128)}, u32[]{:S(2)}, u32[]{:S(2)}) collective-permute-start(s32[1]{0:T(128)} %add.56), channel_id=1, source_target_pairs={{0,96},{16,112},{32,64},{48,80},{64,32},{80,48},{96,0},{112,16},{1... | collective-permute-start | bytes 20 | tf_op jit(solution)/shard_map/ppermute | solution.py:26
  64.9 10.8 %copy-start = (bf16[24,8,64,128]{3,2,1,0:T(8,128)(2,1)S(1)}, bf16[24,8,64,128]{3,2,1,0:T(8,128)(2,1)}, u32[]{:S(2)}) copy-start(bf16[24,8,64,128]{3,2,1,0:T(8,128)(2,1)} %param.34) | copy-start | bytes 9437188
  64.9 10.8 %copy-start.15 = (f32[24,8]{1,0:T(8,128)S(1)}, f32[24,8]{1,0:T(8,128)}, u32[]{:S(2)}) copy-start(f32[24,8]{1,0:T(8,128)} %get-tuple-element.50) | copy-start | bytes 2308
  71.0 7.2 %copy-start.1 = (bf16[4,192,256]{2,1,0:T(8,128)(2,1)}, bf16[4,192,256]{2,1,0:T(8,128)(2,1)S(1)}, u32[]{:S(2)}) copy-start(bf16[4,192,256]{2,1,0:T(8,128)(2,1)S(1)} %add_convert_fusion.1.refs_0_) | copy-start | bytes 1179652
  71.0 8.9 %collective-permute-start.13 = (bf16[4,192,256]{2,1,0:T(8,128)(2,1)S(1)}, bf16[4,192,256]{2,1,0:T(8,128)(2,1)S(1)}, u32[]{:S(2)}, u32[]{:S(2)}) collective-permute-start(bf16[4,192,256]{2,1,0:T(8,128)(2,1)S(1)} %add_convert_fusion.1.refs_0_), channel_id=1, source_target_pairs={{0,5},{1,4},{2,7},{3,6},{4,1},{5,0},{6,3},{7,2},{8,13},{9,12},{10,... | collective-permute-start | bytes 1179656 | tf_op jit(solution)/shard_map/ppermute | solution.py:33
  71.1 12.1 %collective-permute-start.11 = (bf16[4,192,256]{2,1,0:T(8,128)(2,1)S(1)}, bf16[4,192,256]{2,1,0:T(8,128)(2,1)S(1)}, u32[]{:S(2)}, u32[]{:S(2)}) collective-permute-start(bf16[4,192,256]{2,1,0:T(8,128)(2,1)S(1)} %add_convert_fusion.1.refs_0_), channel_id=1, source_target_pairs={{0,4},{1,5},{2,6},{3,7},{4,0},{5,1},{6,2},{7,3},{8,12},{9,13},{10,... | collective-permute-start | bytes 1179656 | tf_op jit(solution)/shard_map/ppermute | solution.py:33
  71.2 12.0 %collective-permute-start.12 = (bf16[4,192,256]{2,1,0:T(8,128)(2,1)S(1)}, bf16[4,192,256]{2,1,0:T(8,128)(2,1)S(1)}, u32[]{:S(2)}, u32[]{:S(2)}) collective-permute-start(bf16[4,192,256]{2,1,0:T(8,128)(2,1)S(1)} %add_convert_fusion.1.refs_0_), channel_id=1, source_target_pairs={{0,1},{1,0},{2,3},{3,2},{4,5},{5,4},{6,7},{7,6},{8,9},{9,8},{10,11... | collective-permute-start | bytes 1179656 | tf_op jit(solution)/shard_map/ppermute | solution.py:33
  79.9 0.8 copy-start.3
  83.2 0.8 copy-start.6
  83.9 0.8 copy-start.7
where the time goes:
time: 88.3 us; the launch traced here: 87.9 us
  Pallas kernels  31.8 us (36%)
  starting transfers between devices  20.3 us (23%)
  waiting for transfers between devices  18.1 us (20%)
  local copies, waits for them, and re-layouts  6.09 us (7%)
  other arithmetic  5.88 us (7%)
  between operations  4.64 us (5%)
  matrix products  1.06 us (1%)
    ppermute x9, waiting for transfers between devices, exchanged(): return lax.ppermute(value, ALL, pairs)  14.4 us
    ppermute x9, starting transfers between devices, exchanged(): return lax.ppermute(value, ALL, pairs)  12.8 us
    pallas_call x1, Pallas kernels, in_project(): pl.pallas_call(body, out_shape=[jax.ShapeDtypeStruct((rows, inner_dev), j...  10.7 us
    pallas_call x2, Pallas kernels, out_project(): pl.pallas_call(body, out_shape=[jax.ShapeDtypeStruct((4, rows, COLS), jnp...  7.59 us
    ppermute x5, starting transfers between devices, swapped(): return lax.ppermute(value, axis, pairs)  7.51 us
    pallas_call x1, Pallas kernels, recur(): pl.pallas_call(body, grid=(requests // each,), out_shape=[jax.ShapeDtypeS...  5.51 us
    pallas_call x2, Pallas kernels, placed(): pl.pallas_call(body, out_shape=jax.ShapeDtypeStruct((rows, 16 * COLS), jn...  4.1 us
    pallas_call x1, Pallas kernels, enter(): pl.pallas_call(body, out_shape=[jax.ShapeDtypeStruct((rows, width), jnp.b...  3.87 us
  transfers between devices with their start and end apart: 14, of which 9 were waited for; matrix products, arithmetic and copies ran while one was open for 8% of the time, Pallas kernels for 18%

commit v1 on v0

--- a/solution.py
+++ b/solution.py
@@ -205,7 +205,7 @@
     depth = half // halves
     viewed = in_weight.reshape(half, 2, 2, lane_blocks, 128).transpose(0, 1, 3, 2, 4)
 
-    def body(normed_ref, weight_ref, gate_ref, value_ref, buffer, left, sems):
+    def body(source_ref, weight_ref, gate_ref, value_ref, normed_ref, buffer, left, sems, sem):
         def copies_of(turn):
             pair, part = turn
             span = pl.ds(part * depth, depth)
@@ -223,6 +223,9 @@
         for turn in turns[:AHEAD]:
             for copy in copies_of(turn):
                 copy.start()
+        entering = pltpu.make_async_copy(source_ref, normed_ref, sem)
+        entering.start()
+        entering.wait()
         flat = buffer.reshape(2 * lane_blocks * width, 128)
         even = lax.broadcasted_iota(jnp.int32, (rows, 128), 1) % 2 == 0
         for lane in range(0, width, 128):
@@ -265,12 +268,14 @@
     return pl.pallas_call(
         body,
         out_shape=[jax.ShapeDtypeStruct((rows, inner_dev), jnp.bfloat16)] * 2,
-        in_specs=[whole, pl.BlockSpec(memory_space=pl.ANY)],
+        in_specs=[pl.BlockSpec(memory_space=pl.ANY)] * 2,
         out_specs=[whole] * 2,
         scratch_shapes=[
+            pltpu.VMEM((rows, width), jnp.bfloat16),
             pltpu.VMEM((2, lane_blocks, half, 2, 128), jnp.bfloat16),
             pltpu.VMEM((2, 2 * rows, width), jnp.bfloat16),
             pltpu.SemaphoreType.DMA((halves, 2, lane_blocks)),
+            pltpu.SemaphoreType.DMA,
         ],
         name="in_project",
     )(normed, viewed)
@@ -458,17 +463,16 @@
     second, first, own = out_project(scaled, out_weight, (2, 1, 0), squares)
     own, value_part, group_proj = lax.optimization_barrier((own, value_part, group_proj))
     received.update(stage({2: second, 1: first}, NEAR, FAR, (2, 1)))
+    kept_count, own = lax.optimization_barrier((kept_count, own))
     count = jnp.sum(kept_count).reshape(1)
-    count, own = lax.optimization_barrier((count, own))
     count = count + swapped(count, DP, 1)
     reduced = added(own, [received[step] for step in (1, 2, 3)])
-    count, reduced = lax.optimization_barrier((count, reduced))
+    count, reduced, weighted = lax.optimization_barrier((count, reduced, weighted))
     count = count + swapped(count, DP, 2)
     received = stage([reduced] * 4, FAR, NEAR)
+    finished = added(reduced, [received[step] for step in (1, 2, 3)])
+    count, finished = lax.optimization_barrier((count, finished))
     accepted_total = count + swapped(count, DP, 6)
-    accepted_total, received[1] = lax.optimization_barrier((accepted_total, received[1]))
-    finished = added(reduced, [received[step] for step in (1, 2, 3)])
-    finished, weighted = lax.optimization_barrier((finished, weighted))
     received = stage([finished] * 4, NEAR, FAR)
     layer_rows = placed([finished, received[3]], (0, 3))
     layer_rows = placed([received[2], received[1]], (2, 1), layer_rows)

time: 88.3 us -> 86.6 us (0.981)
  the two profiles are of different devices: /device:TPU:12 before, /device:TPU:0 now
where the time goes in v1:
time: 86.6 us; the launch traced here: 86.2 us
  Pallas kernels  32.8 us (38%)
  starting transfers between devices  23.8 us (27%)
  waiting for transfers between devices  12 us (14%)
  local copies, waits for them, and re-layouts  6.06 us (7%)
  other arithmetic  5.88 us (7%)
  between operations  4.68 us (5%)
  matrix products  1.05 us (1%)
    ppermute x9, starting transfers between devices, exchanged(): return lax.ppermute(value, ALL, pairs)  13.4 us
    pallas_call x1, Pallas kernels, in_project(): pl.pallas_call(body, out_shape=[jax.ShapeDtypeStruct((rows, inner_dev), j...  11.7 us
    ppermute x5, starting transfers between devices, swapped(): return lax.ppermute(value, axis, pairs)  10.4 us
    ppermute x9, waiting for transfers between devices, exchanged(): return lax.ppermute(value, ALL, pairs)  9.35 us
    pallas_call x2, Pallas kernels, out_project(): pl.pallas_call(body, out_shape=[jax.ShapeDtypeStruct((4, rows, COLS), jnp...  7.64 us
    pallas_call x1, Pallas kernels, recur(): pl.pallas_call(body, grid=(requests // each,), out_shape=[jax.ShapeDtypeS...  5.51 us
    pallas_call x2, Pallas kernels, placed(): pl.pallas_call(body, out_shape=jax.ShapeDtypeStruct((rows, 16 * COLS), jn...  4.1 us
    pallas_call x1, Pallas kernels, enter(): pl.pallas_call(body, out_shape=[jax.ShapeDtypeStruct((rows, width), jnp.b...  3.87 us
  transfers between devices with their start and end apart: 14, of which 8 were waited for; matrix products, arithmetic and copies ran while one was open for 9% of the time, Pallas kernels for 20%

profile of v1, /device:TPU:0, one launch (start us, length us, event | category | flops | bytes accessed | tf_op | source)
XLA Modules:
  0.0 86.2 jit_solution(16927414328722875074)
XLA Ops:
  0.6 3.9 %enter.1 = (bf16[192,4096]{1,0:T(8,128)(2,1)}, bf16[192,128]{1,0:T(8,128)(2,1)}, bf16[24,8,128]{2,1,0:T(8,128)(2,1)}, f32[192,8]{1,0:T(8,128)}) custom-call(bf16[192,4096]{1,0:T(8,128)(2,1)} %bitcast.32, f32[1,4096]{1,0:T(1,128)} %bitcast.38, bf16[4096,128]{1,0:T(8,128)(2,1)} %gw_ref.1, bf16[8,4096]{1,0:T(8,128)(2,1)} %bitcast.36, ...), custom_call_target="tpu_custom_call" | custom-call | tf_op jit(solution)/shard_map/enter/pallas_call | solution.py:184
  4.5 1.7 %collective-permute-start = (bf16[24,8,128]{2,1,0:T(8,128)(2,1)}, bf16[24,8,128]{2,1,0:T(8,128)(2,1)S(1)}, u32[]{:S(2)}, u32[]{:S(2)}) collective-permute-start(bf16[24,8,128]{2,1,0:T(8,128)(2,1)} %get-tuple-element.33.own_ref), channel_id=1, source_target_pairs={{0,1},{1,0},{2,3},{3,2},{4,5},{5,4},{6,7},{7,6},{8,9},{9,8},{10,11... | collective-permute-start | bytes 147464 | tf_op jit(solution)/shard_map/ppermute | solution.py:26
  6.2 11.7 %in_project.1 = (bf16[192,512]{1,0:T(8,128)(2,1)}, bf16[192,512]{1,0:T(8,128)(2,1)}) custom-call(bf16[192,4096]{1,0:T(8,128)(2,1)} %get-tuple-element.29.source_ref, bf16[2048,2,4,2,128]{4,3,2,1,0:T(2,128)(2,1)} %bitcast.30), custom_call_target="tpu_custom_call" | custom-call | tf_op jit(solution)/shard_map/in_project/pallas_call | solution.py:268
  18.5 5.5 %recur.1 = (bf16[192,512]{1,0:T(8,128)(2,1)}, f32[192,1]{1,0:T(8,128)}, bf16[24,8,512]{2,1,0:T(8,128)(2,1)}, f32[24,8]{1,0:T(8,128)}) custom-call(bf16[192,512]{1,0:T(8,128)(2,1)} %get-tuple-element.30.gate_ref, bf16[192,512]{1,0:T(8,128)(2,1)} %get-tuple-element.50.value_ref, bf16[3,24,512]{2,1,0:T(8,128)(2,1)} %bitcast.34, bf16[4,512]{1,0:T(4,128)(2,1)} %ker_ref.3, ...), custom_call_target="tpu_custom_call" | custom-call | tf_op jit(solution)/shard_map/recur/pallas_call | solution.py:365
  24.6 3.3 %out_project.2 = bf16[4,192,256]{2,1,0:T(8,128)(2,1)} custom-call(bf16[192,512]{1,0:T(8,128)(2,1)} %get-tuple-element.36.gated_ref, bf16[512,4096]{1,0:T(8,128)(2,1)} %weight_ref.3), custom_call_target="tpu_custom_call" | custom-call | tf_op jit(solution)/shard_map/out_project/pallas_call | solution.py:86
  28.0 1.1 %collective-permute-done.1.rest_1_ = f32[192,1]{1,0:T(8,128)S(1)} collective-permute-done((f32[192,1]{1,0:T(8,128)}, f32[192,1]{1,0:T(8,128)S(1)}, u32[]{:S(2)}, u32[]{:S(2)}) %collective-permute-start.1) | collective-permute-done | bytes 800 | tf_op jit(solution)/shard_map/ppermute | solution.py:26
  29.3 1.1 %multiply_convert_fusion = bf16[4,192,256]{2,1,0:T(8,128)(2,1)S(1)} fusion(bf16[4,192,256]{2,1,0:T(8,128)(2,1)} %out_project.2, f32[192]{0:T(256)S(1)} %rsqrt_reduce_fusion), kind=kLoop, calls=%fused_computation.5 | loop fusion | flops 589824 | bytes 787200 | tf_op jit(solution)/shard_map/convert_element_type | solution.py:460
  30.4 4.3 %out_project.3 = (bf16[4,192,256]{2,1,0:T(8,128)(2,1)}, bf16[4,192,256]{2,1,0:T(8,128)(2,1)}, bf16[4,192,256]{2,1,0:T(8,128)(2,1)}) custom-call(bf16[192,512]{1,0:T(8,128)(2,1)} %get-tuple-element.36.gated_ref, bf16[512,4096]{1,0:T(8,128)(2,1)} %weight_ref.3, f32[192,1]{1,0:T(8,128)} %get-tuple-element.35.rest_0_, f32[192,1]{1,0:T(8,128)} %copy-done.5), custom_call_target="tpu_custom_call" | custom-call | tf_op jit(solution)/shard_map/out_project/pallas_call | solution.py:86
  34.8 0.7 collective-permute-start.3
  35.4 1.9 %collective-permute-start.4 = (bf16[4,192,256]{2,1,0:T(8,128)(2,1)}, bf16[4,192,256]{2,1,0:T(8,128)(2,1)S(1)}, u32[]{:S(2)}, u32[]{:S(2)}) collective-permute-start(bf16[4,192,256]{2,1,0:T(8,128)(2,1)} %get-tuple-element.43), channel_id=1, source_target_pairs={{0,4},{1,5},{2,6},{3,7},{4,0},{5,1},{6,2},{7,3},{8,12},{9,13},{10,... | collective-permute-start | bytes 1179656 | tf_op jit(solution)/shard_map/ppermute | solution.py:33
  37.4 1.0 %collective-permute-start.5 = (bf16[4,192,256]{2,1,0:T(8,128)(2,1)S(1)}, bf16[4,192,256]{2,1,0:T(8,128)(2,1)S(1)}, u32[]{:S(2)}, u32[]{:S(2)}) collective-permute-start(bf16[4,192,256]{2,1,0:T(8,128)(2,1)S(1)} %multiply_convert_fusion), channel_id=1, source_target_pairs={{0,5},{1,4},{2,7},{3,6},{4,1},{5,0},{6,3},{7,2},{8,13},{9,12},{10,... | collective-permute-start | bytes 1179656 | tf_op jit(solution)/shard_map/ppermute | solution.py:33
  39.0 1.3 %collective-permute-start.2 = (s32[1]{0:T(128)}, s32[1]{0:T(128)}, u32[]{:S(2)}, u32[]{:S(2)}) collective-permute-start(s32[1]{0:T(128)} %bitcast.13), channel_id=1, source_target_pairs={{0,16},{16,0},{32,48},{48,32},{64,80},{80,64},{96,112},{112,96},{1... | collective-permute-start | bytes 20 | tf_op jit(solution)/shard_map/ppermute | solution.py:26
  40.4 0.8 collective-permute-done.2
  42.8 4.3 %collective-permute-done.4 = bf16[4,192,256]{2,1,0:T(8,128)(2,1)S(1)} collective-permute-done((bf16[4,192,256]{2,1,0:T(8,128)(2,1)}, bf16[4,192,256]{2,1,0:T(8,128)(2,1)S(1)}, u32[]{:S(2)}, u32[]{:S(2)}) %collective-permute-start.4) | collective-permute-done | bytes 393248 | tf_op jit(solution)/shard_map/ppermute | solution.py:33
  47.2 1.2 %collective-permute-done.5 = bf16[4,192,256]{2,1,0:T(8,128)(2,1)S(1)} collective-permute-done((bf16[4,192,256]{2,1,0:T(8,128)(2,1)S(1)}, bf16[4,192,256]{2,1,0:T(8,128)(2,1)S(1)}, u32[]{:S(2)}, u32[]{:S(2)}) %collective-permute-start.5) | collective-permute-done | bytes 393248 | tf_op jit(solution)/shard_map/ppermute | solution.py:33
  48.4 1.2 %add_convert_fusion.2 = bf16[4,192,256]{2,1,0:T(8,128)(2,1)S(1)} fusion(bf16[4,192,256]{2,1,0:T(8,128)(2,1)S(1)} %collective-permute-done.5, bf16[4,192,256]{2,1,0:T(8,128)(2,1)S(1)} %collective-permute-done.4, bf16[4,192,256]{2,1,0:T(8,128)(2,1)S(1)} %collective-permute-done.3, bf16[4,192,256]{2,1,0:T(8,128)(2,1)} %get-tuple-element.41), kind=kLoop, calls=%fused_computation.4 | loop fusion | flops 1572864 | bytes 1966080 | tf_op jit(solution)/shard_map/convert_element_type | solution.py:136
  49.6 2.3 %collective-permute-start.7 = (bf16[4,192,256]{2,1,0:T(8,128)(2,1)S(1)}, bf16[4,192,256]{2,1,0:T(8,128)(2,1)S(1)}, u32[]{:S(2)}, u32[]{:S(2)}) collective-permute-start(bf16[4,192,256]{2,1,0:T(8,128)(2,1)S(1)} %add_convert_fusion.2), channel_id=1, source_target_pairs={{0,3},{1,2},{2,1},{3,0},{4,7},{5,6},{6,5},{7,4},{8,11},{9,10},{10,... | collective-permute-start | bytes 1179656 | tf_op jit(solution)/shard_map/ppermute | solution.py:33
  51.8 4.0 %collective-permute-start.8 = (bf16[4,192,256]{2,1,0:T(8,128)(2,1)S(1)}, bf16[4,192,256]{2,1,0:T(8,128)(2,1)S(1)}, u32[]{:S(2)}, u32[]{:S(2)}) collective-permute-start(bf16[4,192,256]{2,1,0:T(8,128)(2,1)S(1)} %add_convert_fusion.2), channel_id=1, source_target_pairs={{0,12},{1,13},{2,14},{3,15},{4,8},{5,9},{6,10},{7,11},{8,4},{9,5},... | collective-permute-start | bytes 1179656 | tf_op jit(solution)/shard_map/ppermute | solution.py:33
  55.8 1.6 %gather_fusion = bf16[24,3,512]{2,0,1:T(8,128)(2,1)} fusion(bf16[24,11,512]{2,0,1:T(8,128)(2,1)S(1)} %pad_maximum_fusion, s32[24]{0:T(128)S(1)} %fusion.7), kind=kCustom, calls=%fused_computation | custom fusion | bytes 147744 | tf_op jit(solution)/shard_map/vmap()/gather | solution.py:394
  57.5 1.4 %gather_fusion.1 = bf16[24,3,128]{2,0,1:T(8,128)(2,1)} fusion(bf16[24,11,128]{2,0,1:T(8,128)(2,1)S(1)} %pad_maximum_fusion.1, s32[24]{0:T(128)S(1)} %fusion.7), kind=kCustom, calls=%fused_computation.1 | custom fusion | bytes 37152 | tf_op jit(solution)/shard_map/vmap()/gather | solution.py:394
  58.9 2.8 %collective-permute-start.6 = (s32[1]{0:T(128)}, s32[1]{0:T(128)}, u32[]{:S(2)}, u32[]{:S(2)}) collective-permute-start(s32[1]{0:T(128)} %add.52), channel_id=1, source_target_pairs={{0,32},{16,48},{32,0},{48,16},{64,96},{80,112},{96,64},{112,80},{1... | collective-permute-start | bytes 20 | tf_op jit(solution)/shard_map/ppermute | solution.py:26
  61.7 1.1 %fusion = f32[24,512,128]{2,1,0:T(8,128)S(1)} fusion(bf16[24,8,512]{2,1,0:T(8,128)(2,1)S(1)} %copy-done.12, bf16[24,8,128]{2,1,0:T(8,128)(2,1)S(1)} %copy-done.9, bf16[24,8,128]{2,1,0:T(8,128)(2,1)S(1)} %copy-done.11, pred[]{:T(512)S(6)} %eq.5), kind=kOutput, calls=%fused_computation.9 | convolution fusion | flops 25190400 | bytes 6586369 | tf_op jit(solution)/shard_map/rjq,rjn->rqn/dot_general | solution.py:481
  63.4 2.0 %collective-permute-done.8 = bf16[4,192,256]{2,1,0:T(8,128)(2,1)S(1)} collective-permute-done((bf16[4,192,256]{2,1,0:T(8,128)(2,1)S(1)}, bf16[4,192,256]{2,1,0:T(8,128)(2,1)S(1)}, u32[]{:S(2)}, u32[]{:S(2)}) %collective-permute-start.8) | collective-permute-done | bytes 393248 | tf_op jit(solution)/shard_map/ppermute | solution.py:33
  65.3 1.6 %collective-permute-done.9 = bf16[4,192,256]{2,1,0:T(8,128)(2,1)S(1)} collective-permute-done((bf16[4,192,256]{2,1,0:T(8,128)(2,1)S(1)}, bf16[4,192,256]{2,1,0:T(8,128)(2,1)S(1)}, u32[]{:S(2)}, u32[]{:S(2)}) %collective-permute-start.9) | collective-permute-done | bytes 393248 | tf_op jit(solution)/shard_map/ppermute | solution.py:33
  67.7 3.0 %collective-permute-start.11 = (bf16[4,192,256]{2,1,0:T(8,128)(2,1)S(1)}, bf16[4,192,256]{2,1,0:T(8,128)(2,1)S(1)}, u32[]{:S(2)}, u32[]{:S(2)}) collective-permute-start(bf16[4,192,256]{2,1,0:T(8,128)(2,1)S(1)} %add_convert_fusion.1.refs_0_), channel_id=1, source_target_pairs={{0,1},{1,0},{2,3},{3,2},{4,5},{5,4},{6,7},{7,6},{8,9},{9,8},{10,11... | collective-permute-start | bytes 1179656 | tf_op jit(solution)/shard_map/ppermute | solution.py:33
  70.7 2.6 %add_convert_fusion = bf16[24,8,64,128]{3,2,1,0:T(8,128)(2,1)} fusion(f32[24,8,64,128]{3,2,1,0:T(8,128)S(1)} %bitcast.28, bf16[24,8,64,128]{3,2,1,0:T(8,128)(2,1)S(1)} %copy-done, f32[24,8]{1,0:T(8,128)S(1)} %copy-done.15), kind=kLoop, calls=%fused_computation.2 | loop fusion | flops 6291456 | bytes 12583680 | tf_op jit(solution)/shard_map/convert_element_type | solution.py:484
  73.3 4.1 %collective-permute-start.13 = (s32[1]{0:T(128)}, s32[1]{0:T(128)}, u32[]{:S(2)}, u32[]{:S(2)}) collective-permute-start(s32[1]{0:T(128)} %add.56), channel_id=1, source_target_pairs={{0,96},{16,112},{32,64},{48,80},{64,32},{80,48},{96,0},{112,16},{1... | collective-permute-start | bytes 20 | tf_op jit(solution)/shard_map/ppermute | solution.py:26
  78.7 0.8 copy-done.3
  79.5 2.0 %place_rows.2.refs_2_ = bf16[192,4096]{1,0:T(8,128)(2,1)} custom-call(bf16[4,192,256]{2,1,0:T(8,128)(2,1)} %copy-done.1, bf16[4,192,256]{2,1,0:T(8,128)(2,1)} %copy-done.3), custom_call_target="tpu_custom_call" | custom-call | tf_op jit(solution)/shard_map/place_rows/pallas_call | solution.py:122
  81.5 0.7 copy-done.6
  82.3 0.8 copy-done.7
  83.0 2.0 %place_rows.3 = bf16[192,4096]{1,0:T(8,128)(2,1)} custom-call(bf16[4,192,256]{2,1,0:T(8,128)(2,1)} %copy-done.6, bf16[4,192,256]{2,1,0:T(8,128)(2,1)} %copy-done.7, bf16[192,4096]{1,0:T(8,128)(2,1)} %place_rows.2.refs_2_), custom_call_target="tpu_custom_call", output_to_operand_aliasing={{}: (2, {})} | custom-call | tf_op jit(solution)/shard_map/place_rows/pallas_call | solution.py:122
  (54 shorter events, 3.8 us)
Async XLA Ops:
  4.5 13.4 %collective-permute-start = (bf16[24,8,128]{2,1,0:T(8,128)(2,1)}, bf16[24,8,128]{2,1,0:T(8,128)(2,1)S(1)}, u32[]{:S(2)}, u32[]{:S(2)}) collective-permute-start(bf16[24,8,128]{2,1,0:T(8,128)(2,1)} %get-tuple-element.33.own_ref), channel_id=1, source_target_pairs={{0,1},{1,0},{2,3},{3,2},{4,5},{5,4},{6,7},{7,6},{8,9},{9,8},{10,11... | collective-permute-start | bytes 147464 | tf_op jit(solution)/shard_map/ppermute | solution.py:26
  17.9 0.6 copy-start.10
  24.0 5.1 %copy-start.4 = (f32[192,1]{1,0:T(8,128)S(1)}, f32[192,1]{1,0:T(8,128)}, u32[]{:S(2)}) copy-start(f32[192,1]{1,0:T(8,128)} %get-tuple-element.35.rest_0_) | copy-start | bytes 2308
  24.0 5.1 %collective-permute-start.1 = (f32[192,1]{1,0:T(8,128)}, f32[192,1]{1,0:T(8,128)S(1)}, u32[]{:S(2)}, u32[]{:S(2)}) collective-permute-start(f32[192,1]{1,0:T(8,128)} %get-tuple-element.35.rest_0_), channel_id=1, source_target_pairs={{0,1},{1,0},{2,3},{3,2},{4,5},{5,4},{6,7},{7,6},{8,9},{9,8},{10,11... | collective-permute-start | bytes 2312 | tf_op jit(solution)/shard_map/ppermute | solution.py:26
  24.6 13.7 %copy-start.16 = (s32[24]{0:T(128)S(1)}, s32[24]{0:T(128)}, u32[]{:S(2)}) copy-start(s32[24]{0:T(128)} %accepted_ref.1) | copy-start | bytes 292
  24.6 13.7 %copy-start.17 = (s32[24]{0:T(128)S(1)}, s32[24]{0:T(128)}, u32[]{:S(2)}) copy-start(s32[24]{0:T(128)} %live_ref.1) | copy-start | bytes 292
  24.6 15.7 %copy-start.2 = (bf16[192,512]{1,0:T(8,128)(2,1)S(1)}, bf16[192,512]{1,0:T(8,128)(2,1)}, u32[]{:S(2)}) copy-start(bf16[192,512]{1,0:T(8,128)(2,1)} %get-tuple-element.50.value_ref) | copy-start | bytes 589828
  28.0 12.4 %copy-start.14 = (bf16[192,128]{1,0:T(8,128)(2,1)S(1)}, bf16[192,128]{1,0:T(8,128)(2,1)}, u32[]{:S(2)}) copy-start(bf16[192,128]{1,0:T(8,128)(2,1)} %get-tuple-element.51) | copy-start | bytes 147460
  28.0 12.4 %copy-start.8 = (bf16[24,3,512]{2,0,1:T(8,128)(2,1)S(1)}, bf16[24,3,512]{2,0,1:T(8,128)(2,1)}, u32[]{:S(2)}) copy-start(bf16[24,3,512]{2,0,1:T(8,128)(2,1)} %param.35) | copy-start | bytes 221188
  29.1 1.3 %copy-start.5 = (f32[192,1]{1,0:T(8,128)}, f32[192,1]{1,0:T(8,128)S(1)}, u32[]{:S(2)}) copy-start(f32[192,1]{1,0:T(8,128)S(1)} %collective-permute-done.1.rest_1_) | copy-start | bytes 2308
  29.2 26.6 %copy-start.13 = (bf16[24,3,128]{2,0,1:T(8,128)(2,1)S(1)}, bf16[24,3,128]{2,0,1:T(8,128)(2,1)}, u32[]{:S(2)}) copy-start(bf16[24,3,128]{2,0,1:T(8,128)(2,1)} %param.36) | copy-start | bytes 55300
  30.4 31.3 %copy-start.9 = (bf16[24,8,128]{2,1,0:T(8,128)(2,1)S(1)}, bf16[24,8,128]{2,1,0:T(8,128)(2,1)}, u32[]{:S(2)}) copy-start(bf16[24,8,128]{2,1,0:T(8,128)(2,1)} %get-tuple-element.33.own_ref) | copy-start | bytes 147460
  30.4 31.3 %copy-start.11 = (bf16[24,8,128]{2,1,0:T(8,128)(2,1)S(1)}, bf16[24,8,128]{2,1,0:T(8,128)(2,1)}, u32[]{:S(2)}) copy-start(bf16[24,8,128]{2,1,0:T(8,128)(2,1)} %copy-done.10) | copy-start | bytes 147460
  30.4 31.3 %copy-start.12 = (bf16[24,8,512]{2,1,0:T(8,128)(2,1)S(1)}, bf16[24,8,512]{2,1,0:T(8,128)(2,1)}, u32[]{:S(2)}) copy-start(bf16[24,8,512]{2,1,0:T(8,128)(2,1)} %get-tuple-element.49) | copy-start | bytes 589828
  34.8 8.1 %collective-permute-start.3 = (bf16[4,192,256]{2,1,0:T(8,128)(2,1)}, bf16[4,192,256]{2,1,0:T(8,128)(2,1)S(1)}, u32[]{:S(2)}, u32[]{:S(2)}) collective-permute-start(bf16[4,192,256]{2,1,0:T(8,128)(2,1)} %get-tuple-element.42), channel_id=1, source_target_pairs={{0,1},{1,0},{2,3},{3,2},{4,5},{5,4},{6,7},{7,6},{8,9},{9,8},{10,11... | collective-permute-start | bytes 1179656 | tf_op jit(solution)/shard_map/ppermute | solution.py:33
  35.4 11.7 %collective-permute-start.4 = (bf16[4,192,256]{2,1,0:T(8,128)(2,1)}, bf16[4,192,256]{2,1,0:T(8,128)(2,1)S(1)}, u32[]{:S(2)}, u32[]{:S(2)}) collective-permute-start(bf16[4,192,256]{2,1,0:T(8,128)(2,1)} %get-tuple-element.43), channel_id=1, source_target_pairs={{0,4},{1,5},{2,6},{3,7},{4,0},{5,1},{6,2},{7,3},{8,12},{9,13},{10,... | collective-permute-start | bytes 1179656 | tf_op jit(solution)/shard_map/ppermute | solution.py:33
  37.4 11.0 %collective-permute-start.5 = (bf16[4,192,256]{2,1,0:T(8,128)(2,1)S(1)}, bf16[4,192,256]{2,1,0:T(8,128)(2,1)S(1)}, u32[]{:S(2)}, u32[]{:S(2)}) collective-permute-start(bf16[4,192,256]{2,1,0:T(8,128)(2,1)S(1)} %multiply_convert_fusion), channel_id=1, source_target_pairs={{0,5},{1,4},{2,7},{3,6},{4,1},{5,0},{6,3},{7,2},{8,13},{9,12},{10,... | collective-permute-start | bytes 1179656 | tf_op jit(solution)/shard_map/ppermute | solution.py:33
  39.0 2.3 %collective-permute-start.2 = (s32[1]{0:T(128)}, s32[1]{0:T(128)}, u32[]{:S(2)}, u32[]{:S(2)}) collective-permute-start(s32[1]{0:T(128)} %bitcast.13), channel_id=1, source_target_pairs={{0,16},{16,0},{32,48},{48,32},{64,80},{80,64},{96,112},{112,96},{1... | collective-permute-start | bytes 20 | tf_op jit(solution)/shard_map/ppermute | solution.py:26
  49.6 13.8 %collective-permute-start.7 = (bf16[4,192,256]{2,1,0:T(8,128)(2,1)S(1)}, bf16[4,192,256]{2,1,0:T(8,128)(2,1)S(1)}, u32[]{:S(2)}, u32[]{:S(2)}) collective-permute-start(bf16[4,192,256]{2,1,0:T(8,128)(2,1)S(1)} %add_convert_fusion.2), channel_id=1, source_target_pairs={{0,3},{1,2},{2,1},{3,0},{4,7},{5,6},{6,5},{7,4},{8,11},{9,10},{10,... | collective-permute-start | bytes 1179656 | tf_op jit(solution)/shard_map/ppermute | solution.py:33
  51.8 13.5 %collective-permute-start.8 = (bf16[4,192,256]{2,1,0:T(8,128)(2,1)S(1)}, bf16[4,192,256]{2,1,0:T(8,128)(2,1)S(1)}, u32[]{:S(2)}, u32[]{:S(2)}) collective-permute-start(bf16[4,192,256]{2,1,0:T(8,128)(2,1)S(1)} %add_convert_fusion.2), channel_id=1, source_target_pairs={{0,12},{1,13},{2,14},{3,15},{4,8},{5,9},{6,10},{7,11},{8,4},{9,5},... | collective-permute-start | bytes 1179656 | tf_op jit(solution)/shard_map/ppermute | solution.py:33
  55.8 11.1 %collective-permute-start.9 = (bf16[4,192,256]{2,1,0:T(8,128)(2,1)S(1)}, bf16[4,192,256]{2,1,0:T(8,128)(2,1)S(1)}, u32[]{:S(2)}, u32[]{:S(2)}) collective-permute-start(bf16[4,192,256]{2,1,0:T(8,128)(2,1)S(1)} %add_convert_fusion.2), channel_id=1, source_target_pairs={{0,15},{1,14},{2,13},{3,12},{4,11},{5,10},{6,9},{7,8},{8,7},{9,6},... | collective-permute-start | bytes 1179656 | tf_op jit(solution)/shard_map/ppermute | solution.py:33
  58.9 11.8 %copy-start = (bf16[24,8,64,128]{3,2,1,0:T(8,128)(2,1)S(1)}, bf16[24,8,64,128]{3,2,1,0:T(8,128)(2,1)}, u32[]{:S(2)}) copy-start(bf16[24,8,64,128]{3,2,1,0:T(8,128)(2,1)} %param.34) | copy-start | bytes 9437188
  58.9 11.8 %copy-start.15 = (f32[24,8]{1,0:T(8,128)S(1)}, f32[24,8]{1,0:T(8,128)}, u32[]{:S(2)}) copy-start(f32[24,8]{1,0:T(8,128)} %get-tuple-element.48) | copy-start | bytes 2308
  58.9 3.9 %collective-permute-start.6 = (s32[1]{0:T(128)}, s32[1]{0:T(128)}, u32[]{:S(2)}, u32[]{:S(2)}) collective-permute-start(s32[1]{0:T(128)} %add.52), channel_id=1, source_target_pairs={{0,32},{16,48},{32,0},{48,16},{64,96},{80,112},{96,64},{112,80},{1... | collective-permute-start | bytes 20 | tf_op jit(solution)/shard_map/ppermute | solution.py:26
  67.1 6.1 %copy-start.1 = (bf16[4,192,256]{2,1,0:T(8,128)(2,1)}, bf16[4,192,256]{2,1,0:T(8,128)(2,1)S(1)}, u32[]{:S(2)}) copy-start(bf16[4,192,256]{2,1,0:T(8,128)(2,1)S(1)} %add_convert_fusion.1.refs_0_) | copy-start | bytes 1179652
  67.1 11.5 %collective-permute-start.12 = (bf16[4,192,256]{2,1,0:T(8,128)(2,1)S(1)}, bf16[4,192,256]{2,1,0:T(8,128)(2,1)S(1)}, u32[]{:S(2)}, u32[]{:S(2)}) collective-permute-start(bf16[4,192,256]{2,1,0:T(8,128)(2,1)S(1)} %add_convert_fusion.1.refs_0_), channel_id=1, source_target_pairs={{0,5},{1,4},{2,7},{3,6},{4,1},{5,0},{6,3},{7,2},{8,13},{9,12},{10,... | collective-permute-start | bytes 1179656 | tf_op jit(solution)/shard_map/ppermute | solution.py:33
  67.2 14.3 %collective-permute-start.10 = (bf16[4,192,256]{2,1,0:T(8,128)(2,1)S(1)}, bf16[4,192,256]{2,1,0:T(8,128)(2,1)S(1)}, u32[]{:S(2)}, u32[]{:S(2)}) collective-permute-start(bf16[4,192,256]{2,1,0:T(8,128)(2,1)S(1)} %add_convert_fusion.1.refs_0_), channel_id=1, source_target_pairs={{0,4},{1,5},{2,6},{3,7},{4,0},{5,1},{6,2},{7,3},{8,12},{9,13},{10,... | collective-permute-start | bytes 1179656 | tf_op jit(solution)/shard_map/ppermute | solution.py:33
  67.7 13.9 %collective-permute-start.11 = (bf16[4,192,256]{2,1,0:T(8,128)(2,1)S(1)}, bf16[4,192,256]{2,1,0:T(8,128)(2,1)S(1)}, u32[]{:S(2)}, u32[]{:S(2)}) collective-permute-start(bf16[4,192,256]{2,1,0:T(8,128)(2,1)S(1)} %add_convert_fusion.1.refs_0_), channel_id=1, source_target_pairs={{0,1},{1,0},{2,3},{3,2},{4,5},{5,4},{6,7},{7,6},{8,9},{9,8},{10,11... | collective-permute-start | bytes 1179656 | tf_op jit(solution)/shard_map/ppermute | solution.py:33
  73.3 4.7 %collective-permute-start.13 = (s32[1]{0:T(128)}, s32[1]{0:T(128)}, u32[]{:S(2)}, u32[]{:S(2)}) collective-permute-start(s32[1]{0:T(128)} %add.56), channel_id=1, source_target_pairs={{0,96},{16,112},{32,64},{48,80},{64,32},{80,48},{96,0},{112,16},{1... | collective-permute-start | bytes 20 | tf_op jit(solution)/shard_map/ppermute | solution.py:26
  78.7 0.8 copy-start.3
  81.5 0.8 copy-start.6
  82.3 0.8 copy-start.7

commit v2 on v1

--- a/solution.py
+++ b/solution.py
@@ -18,7 +18,6 @@
 NEAR = (0, 1, 4, 5)
 FAR = (0, 3, 12, 15)
 COLS = 256
-AHEAD = 2
 
 
 def swapped(value, axis, mask):
@@ -200,32 +199,26 @@
     half = width // 2
     lane_blocks = in_weight.shape[2] // 128
     inner_dev = in_weight.shape[2]
-    pairs = lane_blocks // 2
-    halves = 2
-    depth = half // halves
+    turns = 4
+    depth = half // turns
     viewed = in_weight.reshape(half, 2, 2, lane_blocks, 128).transpose(0, 1, 3, 2, 4)
 
-    def body(source_ref, weight_ref, gate_ref, value_ref, normed_ref, buffer, left, sems, sem):
+    def body(normed_ref, weight_ref, gate_ref, value_ref, buffer, left, sums, sems):
         def copies_of(turn):
-            pair, part = turn
-            span = pl.ds(part * depth, depth)
+            span = pl.ds(turn * depth, depth)
             return [
                 pltpu.make_async_copy(
                     weight_ref.at[span, parity, block],
                     buffer.at[parity, block, span],
-                    sems.at[part, parity, block],
+                    sems.at[turn, parity, block],
                 )
                 for parity in range(2)
-                for block in (2 * pair, 2 * pair + 1)
+                for block in range(lane_blocks)
             ]
 
-        turns = [(pair, part) for pair in range(pairs) for part in range(halves)]
-        for turn in turns[:AHEAD]:
+        for turn in range(turns):
             for copy in copies_of(turn):
                 copy.start()
-        entering = pltpu.make_async_copy(source_ref, normed_ref, sem)
-        entering.start()
-        entering.wait()
         flat = buffer.reshape(2 * lane_blocks * width, 128)
         even = lax.broadcasted_iota(jnp.int32, (rows, 128), 1) % 2 == 0
         for lane in range(0, width, 128):
@@ -237,45 +230,45 @@
             left[0, rows:, span] = pltpu.roll(first, 1, axis=1).astype(jnp.bfloat16)
             left[1, 0:rows, span] = pltpu.roll(second, 127, axis=1).astype(jnp.bfloat16)
             left[1, rows:, span] = second.astype(jnp.bfloat16)
-        total = None
-        for index, (pair, part) in enumerate(turns):
-            for copy in copies_of((pair, part)):
+        for turn in range(turns):
+            for copy in copies_of(turn):
                 copy.wait()
-            if index + AHEAD < len(turns):
-                for copy in copies_of(turns[index + AHEAD]):
-                    copy.start()
+            begin = 2 * depth * turn
+            total = None
             for parity in range(2):
                 right = jnp.concatenate(
                     [
-                        flat[pl.ds((parity * lane_blocks + block) * width + 2 * depth * part, 2 * depth)]
-                        for block in (2 * pair, 2 * pair + 1)
+                        flat[pl.ds((parity * lane_blocks + block) * width + begin, 2 * depth)]
+                        for block in range(lane_blocks)
                     ],
                     axis=1,
                 )
                 product = jnp.dot(
-                    left[parity, :, 2 * depth * part : 2 * depth * (part + 1)],
+                    left[parity, :, begin : begin + 2 * depth],
                     right,
                     preferred_element_type=jnp.float32,
                 )
                 total = product if total is None else total + product
-            if part == halves - 1:
-                span = slice(256 * pair, 256 * pair + 256)
-                gate_ref[:, span] = total[:rows].astype(jnp.bfloat16)
-                value_ref[:, span] = total[rows:].astype(jnp.bfloat16)
-                total = None
+            if turn == 0:
+                sums[...] = total
+            elif turn < turns - 1:
+                sums[...] += total
+            else:
+                total = sums[...] + total
+                gate_ref[...] = total[:rows].astype(jnp.bfloat16)
+                value_ref[...] = total[rows:].astype(jnp.bfloat16)
 
     whole = pl.BlockSpec(memory_space=pltpu.VMEM)
     return pl.pallas_call(
         body,
         out_shape=[jax.ShapeDtypeStruct((rows, inner_dev), jnp.bfloat16)] * 2,
-        in_specs=[pl.BlockSpec(memory_space=pl.ANY)] * 2,
+        in_specs=[whole, pl.BlockSpec(memory_space=pl.ANY)],
         out_specs=[whole] * 2,
         scratch_shapes=[
-            pltpu.VMEM((rows, width), jnp.bfloat16),
             pltpu.VMEM((2, lane_blocks, half, 2, 128), jnp.bfloat16),
             pltpu.VMEM((2, 2 * rows, width), jnp.bfloat16),
-            pltpu.SemaphoreType.DMA((halves, 2, lane_blocks)),
-            pltpu.SemaphoreType.DMA,
+            pltpu.VMEM((2 * rows, inner_dev), jnp.float32),
+            pltpu.SemaphoreType.DMA((turns, 2, lane_blocks)),
         ],
         name="in_project",
     )(normed, viewed)

time: 86.6 us -> 83.3 us (0.962)
  Pallas kernels: 32.8 us -> 29.6 us
    pallas_call x1, Pallas kernels: 11.7 us -> 8.49 us  [in_project(): pl.pallas_call(body, out_shape=[jax.ShapeDtypeStruct((rows, inner_dev), j...]
  transfers between devices with their start and end apart: 14 -> 14, of which waited for: 8 -> 8; matrix products, arithmetic and copies ran while one was open for 9% -> 9% of each run, Pallas kernels for 20% -> 17%
where the time goes in v2:
time: 83.3 us; the launch traced here: 82.8 us
  Pallas kernels  29.6 us (36%)
  starting transfers between devices  23.6 us (28%)
  waiting for transfers between devices  12 us (14%)
  local copies, waits for them, and re-layouts  6.06 us (7%)
  other arithmetic  5.88 us (7%)
  between operations  4.68 us (6%)
  matrix products  1.06 us (1%)
    ppermute x9, starting transfers between devices, exchanged(): return lax.ppermute(value, ALL, pairs)  13.4 us
    ppermute x5, starting transfers between devices, swapped(): return lax.ppermute(value, axis, pairs)  10.2 us
    ppermute x9, waiting for transfers between devices, exchanged(): return lax.ppermute(value, ALL, pairs)  9.36 us
    pallas_call x1, Pallas kernels, in_project(): pl.pallas_call(body, out_shape=[jax.ShapeDtypeStruct((rows, inner_dev), j...  8.49 us
    pallas_call x2, Pallas kernels, out_project(): pl.pallas_call(body, out_shape=[jax.ShapeDtypeStruct((4, rows, COLS), jnp...  7.64 us
    pallas_call x1, Pallas kernels, recur(): pl.pallas_call(body, grid=(requests // each,), out_shape=[jax.ShapeDtypeS...  5.51 us
    pallas_call x2, Pallas kernels, placed(): pl.pallas_call(body, out_shape=jax.ShapeDtypeStruct((rows, 16 * COLS), jn...  4.1 us
    pallas_call x1, Pallas kernels, enter(): pl.pallas_call(body, out_shape=[jax.ShapeDtypeStruct((rows, width), jnp.b...  3.87 us
  transfers between devices with their start and end apart: 14, of which 8 were waited for; matrix products, arithmetic and copies ran while one was open for 9% of the time, Pallas kernels for 17%

profile of v2, /device:TPU:0, one launch (start us, length us, event | category | flops | bytes accessed | tf_op | source)
XLA Modules:
  0.0 82.8 jit_solution(1499454605602741285)
XLA Ops:
  0.6 3.9 %enter.1 = (bf16[192,4096]{1,0:T(8,128)(2,1)}, bf16[192,128]{1,0:T(8,128)(2,1)}, bf16[24,8,128]{2,1,0:T(8,128)(2,1)}, f32[192,8]{1,0:T(8,128)}) custom-call(bf16[192,4096]{1,0:T(8,128)(2,1)} %bitcast.32, f32[1,4096]{1,0:T(1,128)} %bitcast.38, bf16[4096,128]{1,0:T(8,128)(2,1)} %gw_ref.1, bf16[8,4096]{1,0:T(8,128)(2,1)} %bitcast.36, ...), custom_call_target="tpu_custom_call" | custom-call | tf_op jit(solution)/shard_map/enter/pallas_call | solution.py:183
  4.5 1.7 %collective-permute-start = (bf16[24,8,128]{2,1,0:T(8,128)(2,1)}, bf16[24,8,128]{2,1,0:T(8,128)(2,1)S(1)}, u32[]{:S(2)}, u32[]{:S(2)}) collective-permute-start(bf16[24,8,128]{2,1,0:T(8,128)(2,1)} %get-tuple-element.33.own_ref), channel_id=1, source_target_pairs={{0,1},{1,0},{2,3},{3,2},{4,5},{5,4},{6,7},{7,6},{8,9},{9,8},{10,11... | collective-permute-start | bytes 147464 | tf_op jit(solution)/shard_map/ppermute | solution.py:25
  6.2 8.5 %in_project.1 = (bf16[192,512]{1,0:T(8,128)(2,1)}, bf16[192,512]{1,0:T(8,128)(2,1)}) custom-call(bf16[192,4096]{1,0:T(8,128)(2,1)} %get-tuple-element.29.normed_ref, bf16[2048,2,4,2,128]{4,3,2,1,0:T(2,128)(2,1)} %bitcast.30), custom_call_target="tpu_custom_call" | custom-call | tf_op jit(solution)/shard_map/in_project/pallas_call | solution.py:262
  15.3 5.5 %recur.1 = (bf16[192,512]{1,0:T(8,128)(2,1)}, f32[192,1]{1,0:T(8,128)}, bf16[24,8,512]{2,1,0:T(8,128)(2,1)}, f32[24,8]{1,0:T(8,128)}) custom-call(bf16[192,512]{1,0:T(8,128)(2,1)} %get-tuple-element.30.gate_ref, bf16[192,512]{1,0:T(8,128)(2,1)} %get-tuple-element.50.value_ref, bf16[3,24,512]{2,1,0:T(8,128)(2,1)} %bitcast.34, bf16[4,512]{1,0:T(4,128)(2,1)} %ker_ref.3, ...), custom_call_target="tpu_custom_call" | custom-call | tf_op jit(solution)/shard_map/recur/pallas_call | solution.py:358
  21.3 3.3 %out_project.2 = bf16[4,192,256]{2,1,0:T(8,128)(2,1)} custom-call(bf16[192,512]{1,0:T(8,128)(2,1)} %get-tuple-element.36.gated_ref, bf16[512,4096]{1,0:T(8,128)(2,1)} %weight_ref.3), custom_call_target="tpu_custom_call" | custom-call | tf_op jit(solution)/shard_map/out_project/pallas_call | solution.py:85
  24.6 1.1 %collective-permute-done.1.rest_1_ = f32[192,1]{1,0:T(8,128)S(1)} collective-permute-done((f32[192,1]{1,0:T(8,128)}, f32[192,1]{1,0:T(8,128)S(1)}, u32[]{:S(2)}, u32[]{:S(2)}) %collective-permute-start.1) | collective-permute-done | bytes 800 | tf_op jit(solution)/shard_map/ppermute | solution.py:25
  25.9 1.1 %multiply_convert_fusion = bf16[4,192,256]{2,1,0:T(8,128)(2,1)S(1)} fusion(bf16[4,192,256]{2,1,0:T(8,128)(2,1)} %out_project.2, f32[192]{0:T(256)S(1)} %rsqrt_reduce_fusion), kind=kLoop, calls=%fused_computation.5 | loop fusion | flops 589824 | bytes 787200 | tf_op jit(solution)/shard_map/convert_element_type | solution.py:453
  27.1 4.3 %out_project.3 = (bf16[4,192,256]{2,1,0:T(8,128)(2,1)}, bf16[4,192,256]{2,1,0:T(8,128)(2,1)}, bf16[4,192,256]{2,1,0:T(8,128)(2,1)}) custom-call(bf16[192,512]{1,0:T(8,128)(2,1)} %get-tuple-element.36.gated_ref, bf16[512,4096]{1,0:T(8,128)(2,1)} %weight_ref.3, f32[192,1]{1,0:T(8,128)} %get-tuple-element.35.rest_0_, f32[192,1]{1,0:T(8,128)} %copy-done.5), custom_call_target="tpu_custom_call" | custom-call | tf_op jit(solution)/shard_map/out_project/pallas_call | solution.py:85
  32.1 1.9 %collective-permute-start.4 = (bf16[4,192,256]{2,1,0:T(8,128)(2,1)}, bf16[4,192,256]{2,1,0:T(8,128)(2,1)S(1)}, u32[]{:S(2)}, u32[]{:S(2)}) collective-permute-start(bf16[4,192,256]{2,1,0:T(8,128)(2,1)} %get-tuple-element.43), channel_id=1, source_target_pairs={{0,4},{1,5},{2,6},{3,7},{4,0},{5,1},{6,2},{7,3},{8,12},{9,13},{10,... | collective-permute-start | bytes 1179656 | tf_op jit(solution)/shard_map/ppermute | solution.py:32
  34.0 1.0 %collective-permute-start.5 = (bf16[4,192,256]{2,1,0:T(8,128)(2,1)S(1)}, bf16[4,192,256]{2,1,0:T(8,128)(2,1)S(1)}, u32[]{:S(2)}, u32[]{:S(2)}) collective-permute-start(bf16[4,192,256]{2,1,0:T(8,128)(2,1)S(1)} %multiply_convert_fusion), channel_id=1, source_target_pairs={{0,5},{1,4},{2,7},{3,6},{4,1},{5,0},{6,3},{7,2},{8,13},{9,12},{10,... | collective-permute-start | bytes 1179656 | tf_op jit(solution)/shard_map/ppermute | solution.py:32
  35.6 1.3 %collective-permute-start.2 = (s32[1]{0:T(128)}, s32[1]{0:T(128)}, u32[]{:S(2)}, u32[]{:S(2)}) collective-permute-start(s32[1]{0:T(128)} %bitcast.13), channel_id=1, source_target_pairs={{0,16},{16,0},{32,48},{48,32},{64,80},{80,64},{96,112},{112,96},{1... | collective-permute-start | bytes 20 | tf_op jit(solution)/shard_map/ppermute | solution.py:25
  37.1 0.8 collective-permute-done.2
  39.4 4.3 %collective-permute-done.4 = bf16[4,192,256]{2,1,0:T(8,128)(2,1)S(1)} collective-permute-done((bf16[4,192,256]{2,1,0:T(8,128)(2,1)}, bf16[4,192,256]{2,1,0:T(8,128)(2,1)S(1)}, u32[]{:S(2)}, u32[]{:S(2)}) %collective-permute-start.4) | collective-permute-done | bytes 393248 | tf_op jit(solution)/shard_map/ppermute | solution.py:32
  43.8 1.2 %collective-permute-done.5 = bf16[4,192,256]{2,1,0:T(8,128)(2,1)S(1)} collective-permute-done((bf16[4,192,256]{2,1,0:T(8,128)(2,1)S(1)}, bf16[4,192,256]{2,1,0:T(8,128)(2,1)S(1)}, u32[]{:S(2)}, u32[]{:S(2)}) %collective-permute-start.5) | collective-permute-done | bytes 393248 | tf_op jit(solution)/shard_map/ppermute | solution.py:32
  45.0 1.2 %add_convert_fusion.2 = bf16[4,192,256]{2,1,0:T(8,128)(2,1)S(1)} fusion(bf16[4,192,256]{2,1,0:T(8,128)(2,1)S(1)} %collective-permute-done.5, bf16[4,192,256]{2,1,0:T(8,128)(2,1)S(1)} %collective-permute-done.4, bf16[4,192,256]{2,1,0:T(8,128)(2,1)S(1)} %collective-permute-done.3, bf16[4,192,256]{2,1,0:T(8,128)(2,1)} %get-tuple-element.41), kind=kLoop, calls=%fused_computation.4 | loop fusion | flops 1572864 | bytes 1966080 | tf_op jit(solution)/shard_map/convert_element_type | solution.py:135
  46.2 2.2 %collective-permute-start.7 = (bf16[4,192,256]{2,1,0:T(8,128)(2,1)S(1)}, bf16[4,192,256]{2,1,0:T(8,128)(2,1)S(1)}, u32[]{:S(2)}, u32[]{:S(2)}) collective-permute-start(bf16[4,192,256]{2,1,0:T(8,128)(2,1)S(1)} %add_convert_fusion.2), channel_id=1, source_target_pairs={{0,3},{1,2},{2,1},{3,0},{4,7},{5,6},{6,5},{7,4},{8,11},{9,10},{10,... | collective-permute-start | bytes 1179656 | tf_op jit(solution)/shard_map/ppermute | solution.py:32
  48.4 4.0 %collective-permute-start.8 = (bf16[4,192,256]{2,1,0:T(8,128)(2,1)S(1)}, bf16[4,192,256]{2,1,0:T(8,128)(2,1)S(1)}, u32[]{:S(2)}, u32[]{:S(2)}) collective-permute-start(bf16[4,192,256]{2,1,0:T(8,128)(2,1)S(1)} %add_convert_fusion.2), channel_id=1, source_target_pairs={{0,12},{1,13},{2,14},{3,15},{4,8},{5,9},{6,10},{7,11},{8,4},{9,5},... | collective-permute-start | bytes 1179656 | tf_op jit(solution)/shard_map/ppermute | solution.py:32
  52.5 1.6 %gather_fusion = bf16[24,3,512]{2,0,1:T(8,128)(2,1)} fusion(bf16[24,11,512]{2,0,1:T(8,128)(2,1)S(1)} %pad_maximum_fusion, s32[24]{0:T(128)S(1)} %fusion.7), kind=kCustom, calls=%fused_computation | custom fusion | bytes 147744 | tf_op jit(solution)/shard_map/vmap()/gather | solution.py:387
  54.1 1.4 %gather_fusion.1 = bf16[24,3,128]{2,0,1:T(8,128)(2,1)} fusion(bf16[24,11,128]{2,0,1:T(8,128)(2,1)S(1)} %pad_maximum_fusion.1, s32[24]{0:T(128)S(1)} %fusion.7), kind=kCustom, calls=%fused_computation.1 | custom fusion | bytes 37152 | tf_op jit(solution)/shard_map/vmap()/gather | solution.py:387
  55.5 2.8 %collective-permute-start.6 = (s32[1]{0:T(128)}, s32[1]{0:T(128)}, u32[]{:S(2)}, u32[]{:S(2)}) collective-permute-start(s32[1]{0:T(128)} %add.52), channel_id=1, source_target_pairs={{0,32},{16,48},{32,0},{48,16},{64,96},{80,112},{96,64},{112,80},{1... | collective-permute-start | bytes 20 | tf_op jit(solution)/shard_map/ppermute | solution.py:25
  58.3 1.1 %fusion = f32[24,512,128]{2,1,0:T(8,128)S(1)} fusion(bf16[24,8,512]{2,1,0:T(8,128)(2,1)S(1)} %copy-done.12, bf16[24,8,128]{2,1,0:T(8,128)(2,1)S(1)} %copy-done.9, bf16[24,8,128]{2,1,0:T(8,128)(2,1)S(1)} %copy-done.11, pred[]{:T(512)S(6)} %eq.5), kind=kOutput, calls=%fused_computation.9 | convolution fusion | flops 25190400 | bytes 6586369 | tf_op jit(solution)/shard_map/rjq,rjn->rqn/dot_general | solution.py:474
  60.0 1.9 %collective-permute-done.8 = bf16[4,192,256]{2,1,0:T(8,128)(2,1)S(1)} collective-permute-done((bf16[4,192,256]{2,1,0:T(8,128)(2,1)S(1)}, bf16[4,192,256]{2,1,0:T(8,128)(2,1)S(1)}, u32[]{:S(2)}, u32[]{:S(2)}) %collective-permute-start.8) | collective-permute-done | bytes 393248 | tf_op jit(solution)/shard_map/ppermute | solution.py:32
  61.9 1.6 %collective-permute-done.9 = bf16[4,192,256]{2,1,0:T(8,128)(2,1)S(1)} collective-permute-done((bf16[4,192,256]{2,1,0:T(8,128)(2,1)S(1)}, bf16[4,192,256]{2,1,0:T(8,128)(2,1)S(1)}, u32[]{:S(2)}, u32[]{:S(2)}) %collective-permute-start.9) | collective-permute-done | bytes 393248 | tf_op jit(solution)/shard_map/ppermute | solution.py:32
  64.3 3.0 %collective-permute-start.11 = (bf16[4,192,256]{2,1,0:T(8,128)(2,1)S(1)}, bf16[4,192,256]{2,1,0:T(8,128)(2,1)S(1)}, u32[]{:S(2)}, u32[]{:S(2)}) collective-permute-start(bf16[4,192,256]{2,1,0:T(8,128)(2,1)S(1)} %add_convert_fusion.1.refs_0_), channel_id=1, source_target_pairs={{0,1},{1,0},{2,3},{3,2},{4,5},{5,4},{6,7},{7,6},{8,9},{9,8},{10,11... | collective-permute-start | bytes 1179656 | tf_op jit(solution)/shard_map/ppermute | solution.py:32
  67.3 2.6 %add_convert_fusion = bf16[24,8,64,128]{3,2,1,0:T(8,128)(2,1)} fusion(f32[24,8,64,128]{3,2,1,0:T(8,128)S(1)} %bitcast.28, bf16[24,8,64,128]{3,2,1,0:T(8,128)(2,1)S(1)} %copy-done, f32[24,8]{1,0:T(8,128)S(1)} %copy-done.15), kind=kLoop, calls=%fused_computation.2 | loop fusion | flops 6291456 | bytes 12583680 | tf_op jit(solution)/shard_map/convert_element_type | solution.py:477
  69.9 4.1 %collective-permute-start.13 = (s32[1]{0:T(128)}, s32[1]{0:T(128)}, u32[]{:S(2)}, u32[]{:S(2)}) collective-permute-start(s32[1]{0:T(128)} %add.56), channel_id=1, source_target_pairs={{0,96},{16,112},{32,64},{48,80},{64,32},{80,48},{96,0},{112,16},{1... | collective-permute-start | bytes 20 | tf_op jit(solution)/shard_map/ppermute | solution.py:25
  73.9 0.7 collective-permute-done.13
  75.3 0.8 copy-done.3
  76.1 2.0 %place_rows.2.refs_2_ = bf16[192,4096]{1,0:T(8,128)(2,1)} custom-call(bf16[4,192,256]{2,1,0:T(8,128)(2,1)} %copy-done.1, bf16[4,192,256]{2,1,0:T(8,128)(2,1)} %copy-done.3), custom_call_target="tpu_custom_call" | custom-call | tf_op jit(solution)/shard_map/place_rows/pallas_call | solution.py:121
  78.2 0.7 copy-done.6
  78.9 0.8 copy-done.7
  79.7 2.0 %place_rows.3 = bf16[192,4096]{1,0:T(8,128)(2,1)} custom-call(bf16[4,192,256]{2,1,0:T(8,128)(2,1)} %copy-done.6, bf16[4,192,256]{2,1,0:T(8,128)(2,1)} %copy-done.7, bf16[192,4096]{1,0:T(8,128)(2,1)} %place_rows.2.refs_2_), custom_call_target="tpu_custom_call", output_to_operand_aliasing={{}: (2, {})} | custom-call | tf_op jit(solution)/shard_map/place_rows/pallas_call | solution.py:121
  (54 shorter events, 3.6 us)
Async XLA Ops:
  4.5 10.2 %collective-permute-start = (bf16[24,8,128]{2,1,0:T(8,128)(2,1)}, bf16[24,8,128]{2,1,0:T(8,128)(2,1)S(1)}, u32[]{:S(2)}, u32[]{:S(2)}) collective-permute-start(bf16[24,8,128]{2,1,0:T(8,128)(2,1)} %get-tuple-element.33.own_ref), channel_id=1, source_target_pairs={{0,1},{1,0},{2,3},{3,2},{4,5},{5,4},{6,7},{7,6},{8,9},{9,8},{10,11... | collective-permute-start | bytes 147464 | tf_op jit(solution)/shard_map/ppermute | solution.py:25
  14.7 0.6 copy-start.10
  20.8 4.9 %copy-start.4 = (f32[192,1]{1,0:T(8,128)S(1)}, f32[192,1]{1,0:T(8,128)}, u32[]{:S(2)}) copy-start(f32[192,1]{1,0:T(8,128)} %get-tuple-element.35.rest_0_) | copy-start | bytes 2308
  20.8 4.9 %collective-permute-start.1 = (f32[192,1]{1,0:T(8,128)}, f32[192,1]{1,0:T(8,128)S(1)}, u32[]{:S(2)}, u32[]{:S(2)}) collective-permute-start(f32[192,1]{1,0:T(8,128)} %get-tuple-element.35.rest_0_), channel_id=1, source_target_pairs={{0,1},{1,0},{2,3},{3,2},{4,5},{5,4},{6,7},{7,6},{8,9},{9,8},{10,11... | collective-permute-start | bytes 2312 | tf_op jit(solution)/shard_map/ppermute | solution.py:25
  21.3 13.7 %copy-start.16 = (s32[24]{0:T(128)S(1)}, s32[24]{0:T(128)}, u32[]{:S(2)}) copy-start(s32[24]{0:T(128)} %accepted_ref.1) | copy-start | bytes 292
  21.3 13.7 %copy-start.17 = (s32[24]{0:T(128)S(1)}, s32[24]{0:T(128)}, u32[]{:S(2)}) copy-start(s32[24]{0:T(128)} %live_ref.1) | copy-start | bytes 292
  21.3 15.6 %copy-start.2 = (bf16[192,512]{1,0:T(8,128)(2,1)S(1)}, bf16[192,512]{1,0:T(8,128)(2,1)}, u32[]{:S(2)}) copy-start(bf16[192,512]{1,0:T(8,128)(2,1)} %get-tuple-element.50.value_ref) | copy-start | bytes 589828
  24.6 12.4 %copy-start.14 = (bf16[192,128]{1,0:T(8,128)(2,1)S(1)}, bf16[192,128]{1,0:T(8,128)(2,1)}, u32[]{:S(2)}) copy-start(bf16[192,128]{1,0:T(8,128)(2,1)} %get-tuple-element.51) | copy-start | bytes 147460
  24.6 12.4 %copy-start.8 = (bf16[24,3,512]{2,0,1:T(8,128)(2,1)S(1)}, bf16[24,3,512]{2,0,1:T(8,128)(2,1)}, u32[]{:S(2)}) copy-start(bf16[24,3,512]{2,0,1:T(8,128)(2,1)} %param.35) | copy-start | bytes 221188
  25.7 1.3 %copy-start.5 = (f32[192,1]{1,0:T(8,128)}, f32[192,1]{1,0:T(8,128)S(1)}, u32[]{:S(2)}) copy-start(f32[192,1]{1,0:T(8,128)S(1)} %collective-permute-done.1.rest_1_) | copy-start | bytes 2308
  25.9 26.6 %copy-start.13 = (bf16[24,3,128]{2,0,1:T(8,128)(2,1)S(1)}, bf16[24,3,128]{2,0,1:T(8,128)(2,1)}, u32[]{:S(2)}) copy-start(bf16[24,3,128]{2,0,1:T(8,128)(2,1)} %param.36) | copy-start | bytes 55300
  27.0 31.3 %copy-start.9 = (bf16[24,8,128]{2,1,0:T(8,128)(2,1)S(1)}, bf16[24,8,128]{2,1,0:T(8,128)(2,1)}, u32[]{:S(2)}) copy-start(bf16[24,8,128]{2,1,0:T(8,128)(2,1)} %get-tuple-element.33.own_ref) | copy-start | bytes 147460
  27.0 31.3 %copy-start.11 = (bf16[24,8,128]{2,1,0:T(8,128)(2,1)S(1)}, bf16[24,8,128]{2,1,0:T(8,128)(2,1)}, u32[]{:S(2)}) copy-start(bf16[24,8,128]{2,1,0:T(8,128)(2,1)} %copy-done.10) | copy-start | bytes 147460
  27.0 31.3 %copy-start.12 = (bf16[24,8,512]{2,1,0:T(8,128)(2,1)S(1)}, bf16[24,8,512]{2,1,0:T(8,128)(2,1)}, u32[]{:S(2)}) copy-start(bf16[24,8,512]{2,1,0:T(8,128)(2,1)} %get-tuple-element.49) | copy-start | bytes 589828
  31.4 8.1 %collective-permute-start.3 = (bf16[4,192,256]{2,1,0:T(8,128)(2,1)}, bf16[4,192,256]{2,1,0:T(8,128)(2,1)S(1)}, u32[]{:S(2)}, u32[]{:S(2)}) collective-permute-start(bf16[4,192,256]{2,1,0:T(8,128)(2,1)} %get-tuple-element.42), channel_id=1, source_target_pairs={{0,1},{1,0},{2,3},{3,2},{4,5},{5,4},{6,7},{7,6},{8,9},{9,8},{10,11... | collective-permute-start | bytes 1179656 | tf_op jit(solution)/shard_map/ppermute | solution.py:32
  32.1 11.7 %collective-permute-start.4 = (bf16[4,192,256]{2,1,0:T(8,128)(2,1)}, bf16[4,192,256]{2,1,0:T(8,128)(2,1)S(1)}, u32[]{:S(2)}, u32[]{:S(2)}) collective-permute-start(bf16[4,192,256]{2,1,0:T(8,128)(2,1)} %get-tuple-element.43), channel_id=1, source_target_pairs={{0,4},{1,5},{2,6},{3,7},{4,0},{5,1},{6,2},{7,3},{8,12},{9,13},{10,... | collective-permute-start | bytes 1179656 | tf_op jit(solution)/shard_map/ppermute | solution.py:32
  34.0 11.0 %collective-permute-start.5 = (bf16[4,192,256]{2,1,0:T(8,128)(2,1)S(1)}, bf16[4,192,256]{2,1,0:T(8,128)(2,1)S(1)}, u32[]{:S(2)}, u32[]{:S(2)}) collective-permute-start(bf16[4,192,256]{2,1,0:T(8,128)(2,1)S(1)} %multiply_convert_fusion), channel_id=1, source_target_pairs={{0,5},{1,4},{2,7},{3,6},{4,1},{5,0},{6,3},{7,2},{8,13},{9,12},{10,... | collective-permute-start | bytes 1179656 | tf_op jit(solution)/shard_map/ppermute | solution.py:32
  35.6 2.2 %collective-permute-start.2 = (s32[1]{0:T(128)}, s32[1]{0:T(128)}, u32[]{:S(2)}, u32[]{:S(2)}) collective-permute-start(s32[1]{0:T(128)} %bitcast.13), channel_id=1, source_target_pairs={{0,16},{16,0},{32,48},{48,32},{64,80},{80,64},{96,112},{112,96},{1... | collective-permute-start | bytes 20 | tf_op jit(solution)/shard_map/ppermute | solution.py:25
  46.2 13.8 %collective-permute-start.7 = (bf16[4,192,256]{2,1,0:T(8,128)(2,1)S(1)}, bf16[4,192,256]{2,1,0:T(8,128)(2,1)S(1)}, u32[]{:S(2)}, u32[]{:S(2)}) collective-permute-start(bf16[4,192,256]{2,1,0:T(8,128)(2,1)S(1)} %add_convert_fusion.2), channel_id=1, source_target_pairs={{0,3},{1,2},{2,1},{3,0},{4,7},{5,6},{6,5},{7,4},{8,11},{9,10},{10,... | collective-permute-start | bytes 1179656 | tf_op jit(solution)/shard_map/ppermute | solution.py:32
  48.4 13.5 %collective-permute-start.8 = (bf16[4,192,256]{2,1,0:T(8,128)(2,1)S(1)}, bf16[4,192,256]{2,1,0:T(8,128)(2,1)S(1)}, u32[]{:S(2)}, u32[]{:S(2)}) collective-permute-start(bf16[4,192,256]{2,1,0:T(8,128)(2,1)S(1)} %add_convert_fusion.2), channel_id=1, source_target_pairs={{0,12},{1,13},{2,14},{3,15},{4,8},{5,9},{6,10},{7,11},{8,4},{9,5},... | collective-permute-start | bytes 1179656 | tf_op jit(solution)/shard_map/ppermute | solution.py:32
  52.4 11.1 %collective-permute-start.9 = (bf16[4,192,256]{2,1,0:T(8,128)(2,1)S(1)}, bf16[4,192,256]{2,1,0:T(8,128)(2,1)S(1)}, u32[]{:S(2)}, u32[]{:S(2)}) collective-permute-start(bf16[4,192,256]{2,1,0:T(8,128)(2,1)S(1)} %add_convert_fusion.2), channel_id=1, source_target_pairs={{0,15},{1,14},{2,13},{3,12},{4,11},{5,10},{6,9},{7,8},{8,7},{9,6},... | collective-permute-start | bytes 1179656 | tf_op jit(solution)/shard_map/ppermute | solution.py:32
  55.5 11.8 %copy-start = (bf16[24,8,64,128]{3,2,1,0:T(8,128)(2,1)S(1)}, bf16[24,8,64,128]{3,2,1,0:T(8,128)(2,1)}, u32[]{:S(2)}) copy-start(bf16[24,8,64,128]{3,2,1,0:T(8,128)(2,1)} %param.34) | copy-start | bytes 9437188
  55.5 11.8 %copy-start.15 = (f32[24,8]{1,0:T(8,128)S(1)}, f32[24,8]{1,0:T(8,128)}, u32[]{:S(2)}) copy-start(f32[24,8]{1,0:T(8,128)} %get-tuple-element.48) | copy-start | bytes 2308
  55.5 3.9 %collective-permute-start.6 = (s32[1]{0:T(128)}, s32[1]{0:T(128)}, u32[]{:S(2)}, u32[]{:S(2)}) collective-permute-start(s32[1]{0:T(128)} %add.52), channel_id=1, source_target_pairs={{0,32},{16,48},{32,0},{48,16},{64,96},{80,112},{96,64},{112,80},{1... | collective-permute-start | bytes 20 | tf_op jit(solution)/shard_map/ppermute | solution.py:25
  63.7 6.1 %copy-start.1 = (bf16[4,192,256]{2,1,0:T(8,128)(2,1)}, bf16[4,192,256]{2,1,0:T(8,128)(2,1)S(1)}, u32[]{:S(2)}) copy-start(bf16[4,192,256]{2,1,0:T(8,128)(2,1)S(1)} %add_convert_fusion.1.refs_0_) | copy-start | bytes 1179652
  63.7 11.5 %collective-permute-start.12 = (bf16[4,192,256]{2,1,0:T(8,128)(2,1)S(1)}, bf16[4,192,256]{2,1,0:T(8,128)(2,1)S(1)}, u32[]{:S(2)}, u32[]{:S(2)}) collective-permute-start(bf16[4,192,256]{2,1,0:T(8,128)(2,1)S(1)} %add_convert_fusion.1.refs_0_), channel_id=1, source_target_pairs={{0,5},{1,4},{2,7},{3,6},{4,1},{5,0},{6,3},{7,2},{8,13},{9,12},{10,... | collective-permute-start | bytes 1179656 | tf_op jit(solution)/shard_map/ppermute | solution.py:32
  63.8 14.3 %collective-permute-start.10 = (bf16[4,192,256]{2,1,0:T(8,128)(2,1)S(1)}, bf16[4,192,256]{2,1,0:T(8,128)(2,1)S(1)}, u32[]{:S(2)}, u32[]{:S(2)}) collective-permute-start(bf16[4,192,256]{2,1,0:T(8,128)(2,1)S(1)} %add_convert_fusion.1.refs_0_), channel_id=1, source_target_pairs={{0,4},{1,5},{2,6},{3,7},{4,0},{5,1},{6,2},{7,3},{8,12},{9,13},{10,... | collective-permute-start | bytes 1179656 | tf_op jit(solution)/shard_map/ppermute | solution.py:32
  64.3 13.9 %collective-permute-start.11 = (bf16[4,192,256]{2,1,0:T(8,128)(2,1)S(1)}, bf16[4,192,256]{2,1,0:T(8,128)(2,1)S(1)}, u32[]{:S(2)}, u32[]{:S(2)}) collective-permute-start(bf16[4,192,256]{2,1,0:T(8,128)(2,1)S(1)} %add_convert_fusion.1.refs_0_), channel_id=1, source_target_pairs={{0,1},{1,0},{2,3},{3,2},{4,5},{5,4},{6,7},{7,6},{8,9},{9,8},{10,11... | collective-permute-start | bytes 1179656 | tf_op jit(solution)/shard_map/ppermute | solution.py:32
  69.9 4.7 %collective-permute-start.13 = (s32[1]{0:T(128)}, s32[1]{0:T(128)}, u32[]{:S(2)}, u32[]{:S(2)}) collective-permute-start(s32[1]{0:T(128)} %add.56), channel_id=1, source_target_pairs={{0,96},{16,112},{32,64},{48,80},{64,32},{80,48},{96,0},{112,16},{1... | collective-permute-start | bytes 20 | tf_op jit(solution)/shard_map/ppermute | solution.py:25
  75.3 0.8 copy-start.3
  78.1 0.8 copy-start.6
  78.9 0.8 copy-start.7
